TPU v7x, 128 devices: a whole 4x4x4 slice. The times are simulated.
128 devices in a mesh: band: 4 (over y_lo, core), grid: 32 (over x, z, y_hi).
Axes of the slice: x: 4, y: 4 (y_hi: 2, y_lo: 2; y = y_hi * 2 + y_lo), z: 4, core: 2. Of those that a mesh axis runs over, the one named last changes fastest.
Arguments:
- orbitals: bfloat16 [64, 2, 64, 128, 128], P('band', None, 'grid'), may hold values from -1.5 to 1.5
- occupations: float32 [64], P('band'), may hold values from 0.2 to 2
Outputs:
- current: float32 [3, 64, 128, 128], P(None, 'grid', 'band')
All inputs are finite; a program needn't handle non-finite values.
Results may differ from a plain program's by a relative error of at most 0.0003.
Values may be sent and summed in bfloat16 or wider, within the bound.
A program may use at most 64 MiB of HBM per device.

v0:
```python
import math

import jax
import jax.numpy as jnp
from jax import lax
from jax.sharding import PartitionSpec as P


def shifted(block, axis, distance):
    devices = range(lax.axis_size(axis))
    route = [((i - distance) % len(devices), i) for i in devices]
    return lax.ppermute(block, axis, route)


def cut_along(x, dim, peers):
    before, after = (x.shape[:dim], x.shape[dim + 1 :])
    return jnp.moveaxis(x.reshape(*before, peers, -1, *after), dim, 0)


def sum_at_owner(x, axis, dim):
    peers = lax.axis_size(axis)
    tiles = lax.all_to_all(cut_along(x, dim, peers), axis, 0, 0, tiled=True)
    return jnp.sum(tiles, axis=0)


def derivative(values, direction):
    forward = jnp.roll(values, -1, direction) - jnp.roll(values, 1, direction)
    farther = jnp.roll(values, -2, direction) - jnp.roll(values, 2, direction)
    return (8.0 * forward - farther) / 12.0


def vertical(widened, depth_cells):
    forward = widened[:, 3 : 3 + depth_cells] - widened[:, 1 : 1 + depth_cells]
    farther = widened[:, 4 : 4 + depth_cells] - widened[:, 0:depth_cells]
    return (8.0 * forward - farther) / 12.0


def band_sum(orbitals, weights, with_depth, lateral):
    bands = orbitals.shape[0]
    depth_cells = orbitals.shape[2]
    block_size = math.gcd(bands, 8)
    parts_count = (1 if with_depth else 0) + (2 if lateral else 0)

    def advance(block_index, summed):
        offset = block_index * block_size
        center = lax.dynamic_slice_in_dim(orbitals, offset, block_size, 0).astype(jnp.float32)
        factors = lax.dynamic_slice_in_dim(weights, offset, block_size, 0)
        real_part = center[:, 0]
        imag_part = center[:, 1]
        terms = []
        if with_depth:
            widened = jnp.pad(center, ((0, 0), (0, 0), (2, 2), (0, 0), (0, 0)))
            terms.append(
                real_part * vertical(widened[:, 1], depth_cells)
                - imag_part * vertical(widened[:, 0], depth_cells)
            )
        if lateral:
            for direction in (2, 3):
                terms.append(
                    real_part * derivative(imag_part, direction)
                    - imag_part * derivative(real_part, direction)
                )
        stacked = jnp.stack(terms)
        return summed + jnp.sum(factors[None, :, None, None, None] * stacked, 1)

    initial = jnp.zeros(
        (parts_count, depth_cells, orbitals.shape[3], orbitals.shape[4]), jnp.float32
    )
    return lax.fori_loop(0, bands // block_size, advance, initial)


def pair_term(first, second, weights):
    return jnp.sum(
        weights[:, None, None] * (first[:, 0] * second[:, 1] - first[:, 1] * second[:, 0]), 0
    )


def depth_part(orbitals, weights):
    local_sums = band_sum(orbitals, weights, True, False)
    lower_rim = shifted(orbitals, "grid", 1).astype(jnp.float32)
    bottom = orbitals.astype(jnp.float32)
    pair_near = pair_term(lower_rim[:, :, 1], bottom[:, :, 0], weights)
    pair_skip = pair_term(lower_rim[:, :, 1], bottom[:, :, 1], weights)
    pair_far = pair_term(lower_rim[:, :, 0], bottom[:, :, 0], weights)
    upper_terms = jnp.stack([-pair_far / 12.0, (8.0 * pair_near - pair_skip) / 12.0])
    returned = shifted(upper_terms, "grid", -1)
    lower_terms = jnp.stack([(8.0 * pair_near - pair_far) / 12.0, -pair_skip / 12.0])
    depth_cells = orbitals.shape[2]
    boundary = jnp.zeros(local_sums.shape[1:], jnp.float32)
    boundary = boundary.at[0:2].add(lower_terms)
    boundary = boundary.at[depth_cells - 2 :].add(returned)
    return local_sums.at[0].add(boundary)


def per_device(orbitals, occupations):
    lateral_part = band_sum(orbitals, occupations, False, True)
    plane_sums = sum_at_owner(lateral_part, "band", 2)
    depth_sums = sum_at_owner(depth_part(orbitals, occupations), "band", 2)
    return jnp.concatenate([depth_sums, plane_sums], 0)


def solution(mesh):
    placed = (P("band", None, "grid", None, None), P("band"))
    return jax.shard_map(
        per_device,
        mesh=mesh,
        in_specs=placed,
        out_specs=P(None, "grid", "band", None),
        check_vma=False,
    )
```

profile of v0, /device:TPU:1, one launch (start us, length us, event | category | flops | bytes accessed | tf_op | source)
XLA Modules:
  0.0 101.6 jit_solution(4731620502977543177)
XLA Ops:
  0.0 3.7 %collective-permute-start = (bf16[16,2,2,128,128]{4,3,2,1,0:T(8,128)(2,1)}, bf16[16,2,2,128,128]{4,3,2,1,0:T(8,128)(2,1)}, u32[]{:S(2)}, u32[]{:S(2)}) collective-permute-start(bf16[16,2,2,128,128]{4,3,2,1,0:T(8,128)(2,1)} %param.16), channel_id=1, source_target_pairs={{31,0},{0,1},{1,2},{2,3},{3,4},{4,5},{5,6},{6,7},{7,8},{8,9},{9,10... | collective-permute-start | bytes 6291464 | tf_op jit(solution)/shard_map/ppermute | solution.py:12
  3.7 67.3 %while.36 = (s32[]{:T(128)}, f32[2,2,128,128]{3,2,1,0:T(8,128)S(1)}, f32[16]{0:T(128)}, bf16[16,2,2,128,128]{4,3,2,1,0:T(8,128)(2,1)}, s32[]{:T(128)}, /*index=5*/s32[]{:T(128)}, s32[]{:T(128)}, s32[]{:T(128)}) while((s32[]{:T(128)}, f32[2,2,128,128]{3,2,1,0:T(8,128)S(1)}, f32[16]{0:T(128)}, ...), condition=%wide.region_9.10_spmd.clone, body=%wide.region_7.9_spmd.clone.sunk | while | flops 13172743 | bytes 86114896 | solution.py:69
  7.0 2.3 %fusion.62 = (f32[8,2,128,1]{3,0,2,1:T(8,128)}, f32[8,2,128,1]{3,0,2,1:T(8,128)}, f32[8,2,128,1]{3,0,2,1:T(8,128)S(1)}, f32[8,2,128,1]{3,0,2,1:T(8,128)}) fusion(f32[8,2,128,128]{3,0,2,1:T(8,128)S(1)} %get-tuple-element.459, f32[8,2,128,128]{3,0,2,1:T(8,128)S(1)} %get-tuple-element.460), kind=kLoop, calls=%fused_computation.114.clone.1 | loop fusion | bytes 65536 | tf_op jit(solution)/shard_map/while/body/eval_jaxpr/jit(_roll_static)/slice | solution.py:27
  10.1 2.6 %slice_bitcast_fusion.45 = (f32[1,8,2,128,127]{4,1,3,2,0:T(8,128)}, f32[1,8,2,128,127]{4,1,3,2,0:T(8,128)}, f32[1,8,2,128,127]{4,1,3,2,0:T(8,128)}, f32[1,8,2,128,127]{4,1,3,2,0:T(8,128)}) fusion(f32[8,2,128,128]{3,0,2,1:T(8,128)S(1)} %get-tuple-element.459, f32[8,2,128,128]{3,0,2,1:T(8,128)S(1)} %get-tuple-element.460), kind=kLoop, calls=%fused_computation.29.clone.1 | loop fusion | bytes 8323072 | tf_op jit(solution)/shard_map/while/body/eval_jaxpr/jit(_roll_static)/concatenate | solution.py:27
  12.7 1.6 %copy.107 = f32[8,2,128,1]{2,0,3,1:T(8,128)S(1)} copy(f32[8,2,128,1]{3,0,2,1:T(8,128)} %get-tuple-element.464) | data formatting | bytes 16384 | tf_op jit(solution)/shard_map/while/body/eval_jaxpr/jit(_roll_static)/slice | solution.py:27
  14.2 1.4 %copy.108 = f32[1,8,2,128,1]{4,1,3,2,0:T(8,128)} copy(f32[1,8,2,128,1]{3,1,4,2,0:T(8,128)S(1)} %bitcast.183) | data formatting | bytes 16384 | tf_op jit(solution)/shard_map/while/body/eval_jaxpr/jit(_roll_static)/concatenate | solution.py:27
  15.6 2.6 %slice_bitcast_fusion.46 = (f32[1,8,2,128,2]{4,1,3,2,0:T(8,128)}, f32[1,8,2,128,2]{4,1,3,2,0:T(8,128)}, f32[1,8,2,128,2]{4,1,3,2,0:T(8,128)}, f32[1,8,2,128,2]{4,1,3,2,0:T(8,128)}) fusion(f32[8,2,128,128]{3,0,2,1:T(8,128)S(1)} %get-tuple-element.459, f32[8,2,128,128]{3,0,2,1:T(8,128)S(1)} %get-tuple-element.460), kind=kLoop, calls=%fused_computation.26.clone.1 | loop fusion | bytes 131072 | tf_op jit(solution)/shard_map/while/body/eval_jaxpr/jit(_roll_static)/concatenate | solution.py:28
  18.2 2.6 %slice_bitcast_fusion.47 = (f32[1,8,2,128,126]{4,1,3,2,0:T(8,128)}, f32[1,8,2,128,126]{4,1,3,2,0:T(8,128)}, f32[1,8,2,128,126]{4,1,3,2,0:T(8,128)}, f32[1,8,2,128,126]{4,1,3,2,0:T(8,128)}) fusion(f32[8,2,128,128]{3,0,2,1:T(8,128)S(1)} %get-tuple-element.459, f32[8,2,128,128]{3,0,2,1:T(8,128)S(1)} %get-tuple-element.460), kind=kLoop, calls=%fused_computation.25.clone.1 | loop fusion | bytes 8257536 | tf_op jit(solution)/shard_map/while/body/eval_jaxpr/jit(_roll_static)/concatenate | solution.py:28
  20.8 1.6 %copy.109 = f32[8,2,128,1]{2,0,3,1:T(8,128)S(1)} copy(f32[8,2,128,1]{3,0,2,1:T(8,128)} %get-tuple-element.469) | data formatting | bytes 16384 | tf_op jit(solution)/shard_map/while/body/eval_jaxpr/jit(_roll_static)/slice | solution.py:27
  22.4 1.4 %copy.110 = f32[1,8,2,128,1]{4,1,3,2,0:T(8,128)} copy(f32[1,8,2,128,1]{3,1,4,2,0:T(8,128)S(1)} %bitcast.184) | data formatting | bytes 16384 | tf_op jit(solution)/shard_map/while/body/eval_jaxpr/jit(_roll_static)/concatenate | solution.py:27
  23.7 1.6 %copy.111 = f32[8,2,128,1]{2,0,3,1:T(8,128)S(1)} copy(f32[8,2,128,1]{3,0,2,1:T(8,128)} %get-tuple-element.472) | data formatting | bytes 16384 | tf_op jit(solution)/shard_map/while/body/eval_jaxpr/jit(_roll_static)/slice | solution.py:27
  25.3 1.4 %copy.112 = f32[1,8,2,128,1]{4,1,3,2,0:T(8,128)} copy(f32[1,8,2,128,1]{3,1,4,2,0:T(8,128)S(1)} %bitcast.185) | data formatting | bytes 16384 | tf_op jit(solution)/shard_map/while/body/eval_jaxpr/jit(_roll_static)/concatenate | solution.py:27
  26.7 7.3 %fusion.63 = f32[1,8,2,128,128]{4,1,3,2,0:T(8,128)S(1)} fusion(f32[1,8,2,128,1]{4,1,3,2,0:T(8,128)S(1)} %copy.106, f32[1,8,2,128,127]{4,1,3,2,0:T(8,128)} %get-tuple-element.462, f32[1,8,2,128,127]{4,1,3,2,0:T(8,128)} %get-tuple-element.463, f32[1,8,2,128,1]{4,1,3,2,0:T(8,128)} %copy.108, f32[1,8,2,128,2]{4,1,3,2,0:T(8,128)} %get-tuple-element.465, ...), kind=kLoop, calls=%fused_computation.55.clone.1 | loop fusion | flops 5505024 | bytes 11534336 | tf_op jit(solution)/shard_map/while/body/eval_jaxpr/sub | solution.py:60
  40.6 2.3 %fusion.62 = (f32[8,2,128,1]{3,0,2,1:T(8,128)}, f32[8,2,128,1]{3,0,2,1:T(8,128)}, f32[8,2,128,1]{3,0,2,1:T(8,128)S(1)}, f32[8,2,128,1]{3,0,2,1:T(8,128)}) fusion(f32[8,2,128,128]{3,0,2,1:T(8,128)S(1)} %get-tuple-element.459, f32[8,2,128,128]{3,0,2,1:T(8,128)S(1)} %get-tuple-element.460), kind=kLoop, calls=%fused_computation.114.clone.1 | loop fusion | bytes 65536 | tf_op jit(solution)/shard_map/while/body/eval_jaxpr/jit(_roll_static)/slice | solution.py:27
  43.7 2.6 %slice_bitcast_fusion.45 = (f32[1,8,2,128,127]{4,1,3,2,0:T(8,128)}, f32[1,8,2,128,127]{4,1,3,2,0:T(8,128)}, f32[1,8,2,128,127]{4,1,3,2,0:T(8,128)}, f32[1,8,2,128,127]{4,1,3,2,0:T(8,128)}) fusion(f32[8,2,128,128]{3,0,2,1:T(8,128)S(1)} %get-tuple-element.459, f32[8,2,128,128]{3,0,2,1:T(8,128)S(1)} %get-tuple-element.460), kind=kLoop, calls=%fused_computation.29.clone.1 | loop fusion | bytes 8323072 | tf_op jit(solution)/shard_map/while/body/eval_jaxpr/jit(_roll_static)/concatenate | solution.py:27
  46.3 1.6 %copy.107 = f32[8,2,128,1]{2,0,3,1:T(8,128)S(1)} copy(f32[8,2,128,1]{3,0,2,1:T(8,128)} %get-tuple-element.464) | data formatting | bytes 16384 | tf_op jit(solution)/shard_map/while/body/eval_jaxpr/jit(_roll_static)/slice | solution.py:27
  47.9 1.4 %copy.108 = f32[1,8,2,128,1]{4,1,3,2,0:T(8,128)} copy(f32[1,8,2,128,1]{3,1,4,2,0:T(8,128)S(1)} %bitcast.183) | data formatting | bytes 16384 | tf_op jit(solution)/shard_map/while/body/eval_jaxpr/jit(_roll_static)/concatenate | solution.py:27
  49.2 2.6 %slice_bitcast_fusion.46 = (f32[1,8,2,128,2]{4,1,3,2,0:T(8,128)}, f32[1,8,2,128,2]{4,1,3,2,0:T(8,128)}, f32[1,8,2,128,2]{4,1,3,2,0:T(8,128)}, f32[1,8,2,128,2]{4,1,3,2,0:T(8,128)}) fusion(f32[8,2,128,128]{3,0,2,1:T(8,128)S(1)} %get-tuple-element.459, f32[8,2,128,128]{3,0,2,1:T(8,128)S(1)} %get-tuple-element.460), kind=kLoop, calls=%fused_computation.26.clone.1 | loop fusion | bytes 131072 | tf_op jit(solution)/shard_map/while/body/eval_jaxpr/jit(_roll_static)/concatenate | solution.py:28
  51.9 2.6 %slice_bitcast_fusion.47 = (f32[1,8,2,128,126]{4,1,3,2,0:T(8,128)}, f32[1,8,2,128,126]{4,1,3,2,0:T(8,128)}, f32[1,8,2,128,126]{4,1,3,2,0:T(8,128)}, f32[1,8,2,128,126]{4,1,3,2,0:T(8,128)}) fusion(f32[8,2,128,128]{3,0,2,1:T(8,128)S(1)} %get-tuple-element.459, f32[8,2,128,128]{3,0,2,1:T(8,128)S(1)} %get-tuple-element.460), kind=kLoop, calls=%fused_computation.25.clone.1 | loop fusion | bytes 8257536 | tf_op jit(solution)/shard_map/while/body/eval_jaxpr/jit(_roll_static)/concatenate | solution.py:28
  54.5 1.6 %copy.109 = f32[8,2,128,1]{2,0,3,1:T(8,128)S(1)} copy(f32[8,2,128,1]{3,0,2,1:T(8,128)} %get-tuple-element.469) | data formatting | bytes 16384 | tf_op jit(solution)/shard_map/while/body/eval_jaxpr/jit(_roll_static)/slice | solution.py:27
  56.0 1.4 %copy.110 = f32[1,8,2,128,1]{4,1,3,2,0:T(8,128)} copy(f32[1,8,2,128,1]{3,1,4,2,0:T(8,128)S(1)} %bitcast.184) | data formatting | bytes 16384 | tf_op jit(solution)/shard_map/while/body/eval_jaxpr/jit(_roll_static)/concatenate | solution.py:27
  57.4 1.6 %copy.111 = f32[8,2,128,1]{2,0,3,1:T(8,128)S(1)} copy(f32[8,2,128,1]{3,0,2,1:T(8,128)} %get-tuple-element.472) | data formatting | bytes 16384 | tf_op jit(solution)/shard_map/while/body/eval_jaxpr/jit(_roll_static)/slice | solution.py:27
  58.9 1.4 %copy.112 = f32[1,8,2,128,1]{4,1,3,2,0:T(8,128)} copy(f32[1,8,2,128,1]{3,1,4,2,0:T(8,128)S(1)} %bitcast.185) | data formatting | bytes 16384 | tf_op jit(solution)/shard_map/while/body/eval_jaxpr/jit(_roll_static)/concatenate | solution.py:27
  60.4 7.3 %fusion.63 = f32[1,8,2,128,128]{4,1,3,2,0:T(8,128)S(1)} fusion(f32[1,8,2,128,1]{4,1,3,2,0:T(8,128)S(1)} %copy.106, f32[1,8,2,128,127]{4,1,3,2,0:T(8,128)} %get-tuple-element.462, f32[1,8,2,128,127]{4,1,3,2,0:T(8,128)} %get-tuple-element.463, f32[1,8,2,128,1]{4,1,3,2,0:T(8,128)} %copy.108, f32[1,8,2,128,2]{4,1,3,2,0:T(8,128)} %get-tuple-element.465, ...), kind=kLoop, calls=%fused_computation.55.clone.1 | loop fusion | flops 5505024 | bytes 11534336 | tf_op jit(solution)/shard_map/while/body/eval_jaxpr/sub | solution.py:60
  71.8 4.3 %all-to-all-start.1 = ((f32[4,2,2,32,128]{4,3,2,1,0:T(8,128)}), f32[4,2,2,32,128]{4,3,2,1,0:T(8,128)S(1)}, u32[]{:S(2)}, u32[]{:S(2)}) async-start(f32[4,2,2,32,128]{4,3,2,1,0:T(8,128)} %copy.80), calls=%async_computation.1 | async-start | bytes 524288 | tf_op jit(solution)/shard_map/all_to_all | solution.py:22
  76.1 2.1 %copy_convert_fusion.1 = f32[16,2,2,128,128]{4,3,0,1,2:T(8,128)S(1)} fusion(bf16[16,2,2,128,128]{4,3,2,1,0:T(8,128)(2,1)} %get-tuple-element.542), kind=kLoop, calls=%fused_computation.88 | loop fusion | flops 1048576 | bytes 6291456 | tf_op jit(solution)/shard_map/convert_element_type | solution.py:81
  78.5 2.1 %convert_element_type.31 = f32[16,2,2,128,128]{4,3,2,1,0:T(8,128)S(1)} convert(bf16[16,2,2,128,128]{4,3,2,1,0:T(8,128)(2,1)} %collective-permute-done) | non-fusion elementwise | flops 1048576 | bytes 6291456 | tf_op jit(solution)/shard_map/convert_element_type | solution.py:80
  80.8 1.5 %copy_bitcast_fusion = f32[16,2,128,128]{3,2,0,1:T(8,128)S(1)} fusion(bf16[16,2,2,128,128]{4,3,2,1,0:T(8,128)(2,1)} %collective-permute-done), kind=kLoop, calls=%fused_computation.87 | loop fusion | bytes 4194304 | tf_op jit(solution)/shard_map/squeeze | solution.py:82
  83.4 5.5 %collective-permute-start.1 = (f32[2,128,128]{2,1,0:T(8,128)S(1)}, f32[2,128,128]{2,1,0:T(8,128)S(1)}, u32[]{:S(2)}, u32[]{:S(2)}) collective-permute-start(f32[2,128,128]{2,1,0:T(8,128)S(1)} %pad_maximum_fusion), channel_id=1, source_target_pairs={{1,0},{2,1},{3,2},{4,3},{5,4},{6,5},{7,6},{8,7},{9,8},{10,9},{11,1... | collective-permute-start | bytes 393224 | tf_op jit(solution)/shard_map/ppermute | solution.py:12
  88.9 4.2 %while.35 = (s32[]{:T(128)}, f32[1,2,128,128]{3,2,1,0:T(8,128)S(1)}, f32[16]{0:T(128)S(1)}, bf16[16,2,2,128,128]{4,3,2,1,0:T(8,128)(2,1)S(1)}, s32[]{:T(128)}, /*index=5*/s32[]{:T(128)}, s32[]{:T(128)}, s32[]{:T(128)}) while((s32[]{:T(128)}, f32[1,2,128,128]{3,2,1,0:T(8,128)S(1)}, f32[16]{0:T(128)S(1)}, ...), condition=%wide.region_2.3_spmd.clone, body=%wide.region_0.2_spmd.clone.sunk | while | flops 5013511 | bytes 21496064 | solution.py:69
  93.8 3.6 %all-to-all-start = ((f32[4,1,2,32,128]{4,3,2,1,0:T(8,128)}), f32[4,1,2,32,128]{4,3,2,1,0:T(8,128)S(1)}, u32[]{:S(2)}, u32[]{:S(2)}) async-start(f32[4,1,2,32,128]{4,3,2,1,0:T(8,128)} %copy.78), calls=%async_computation | async-start | bytes 262144 | tf_op jit(solution)/shard_map/all_to_all | solution.py:22
  97.4 3.5 %all-to-all-done = f32[4,1,2,32,128]{4,3,2,1,0:T(8,128)S(1)} async-done(((f32[4,1,2,32,128]{4,3,2,1,0:T(8,128)}), f32[4,1,2,32,128]{4,3,2,1,0:T(8,128)S(1)}, u32[]{:S(2)}, u32[]{:S(2)}) %all-to-all-start) | async-done | bytes 131104 | tf_op jit(solution)/shard_map/all_to_all | solution.py:22
  (68 shorter events, 22.4 us)
Async XLA Ops:
  0.0 78.5 %collective-permute-start = (bf16[16,2,2,128,128]{4,3,2,1,0:T(8,128)(2,1)}, bf16[16,2,2,128,128]{4,3,2,1,0:T(8,128)(2,1)}, u32[]{:S(2)}, u32[]{:S(2)}) collective-permute-start(bf16[16,2,2,128,128]{4,3,2,1,0:T(8,128)(2,1)} %param.16), channel_id=1, source_target_pairs={{31,0},{0,1},{1,2},{2,3},{3,4},{4,5},{5,6},{6,7},{7,8},{8,9},{9,10... | collective-permute-start | bytes 6291464 | tf_op jit(solution)/shard_map/ppermute | solution.py:12
  5.7 1.3 %copy-start = (f32[8,2,2,128,128]{4,0,3,2,1:T(8,128)}, f32[8,2,2,128,128]{4,0,3,2,1:T(8,128)S(1)}, u32[]{:S(2)}) copy-start(f32[8,2,2,128,128]{4,0,3,2,1:T(8,128)S(1)} %copy_convert_fusion.3) | copy-start | bytes 6291460 | tf_op jit(solution)/shard_map/while
  34.3 1.6 %copy-start.1 = (f32[8,2,2,128,128]{4,0,3,2,1:T(8,128)S(1)}, f32[8,2,2,128,128]{4,0,3,2,1:T(8,128)}, u32[]{:S(2)}) copy-start(f32[8,2,2,128,128]{4,0,3,2,1:T(8,128)} %copy-done) | copy-start | bytes 6291460 | tf_op jit(solution)/shard_map/while
  35.9 0.7 copy-start.3
  39.3 1.3 %copy-start = (f32[8,2,2,128,128]{4,0,3,2,1:T(8,128)}, f32[8,2,2,128,128]{4,0,3,2,1:T(8,128)S(1)}, u32[]{:S(2)}) copy-start(f32[8,2,2,128,128]{4,0,3,2,1:T(8,128)S(1)} %copy_convert_fusion.3) | copy-start | bytes 6291460 | tf_op jit(solution)/shard_map/while
  68.0 1.6 %copy-start.1 = (f32[8,2,2,128,128]{4,0,3,2,1:T(8,128)S(1)}, f32[8,2,2,128,128]{4,0,3,2,1:T(8,128)}, u32[]{:S(2)}) copy-start(f32[8,2,2,128,128]{4,0,3,2,1:T(8,128)} %copy-done) | copy-start | bytes 6291460 | tf_op jit(solution)/shard_map/while
  69.5 0.7 copy-start.3
  71.8 22.0 %all-to-all-start.1 = ((f32[4,2,2,32,128]{4,3,2,1,0:T(8,128)}), f32[4,2,2,32,128]{4,3,2,1,0:T(8,128)S(1)}, u32[]{:S(2)}, u32[]{:S(2)}) async-start(f32[4,2,2,32,128]{4,3,2,1,0:T(8,128)} %copy.80), calls=%async_computation.1 | async-start | bytes 524288 | tf_op jit(solution)/shard_map/all_to_all | solution.py:22
  80.8 1.5 %copy-start.4 = (f32[16]{0:T(128)S(1)}, f32[16]{0:T(128)}, u32[]{:S(2)}) copy-start(f32[16]{0:T(128)} %get-tuple-element.547) | copy-start | bytes 196
  82.3 6.6 %copy-start.2 = (bf16[16,2,2,128,128]{4,3,2,1,0:T(8,128)(2,1)S(1)}, bf16[16,2,2,128,128]{4,3,2,1,0:T(8,128)(2,1)}, u32[]{:S(2)}) copy-start(bf16[16,2,2,128,128]{4,3,2,1,0:T(8,128)(2,1)} %get-tuple-element.542) | copy-start | bytes 6291460
  83.4 9.7 %collective-permute-start.1 = (f32[2,128,128]{2,1,0:T(8,128)S(1)}, f32[2,128,128]{2,1,0:T(8,128)S(1)}, u32[]{:S(2)}, u32[]{:S(2)}) collective-permute-start(f32[2,128,128]{2,1,0:T(8,128)S(1)} %pad_maximum_fusion), channel_id=1, source_target_pairs={{1,0},{2,1},{3,2},{4,3},{5,4},{6,5},{7,6},{8,7},{9,8},{10,9},{11,1... | collective-permute-start | bytes 393224 | tf_op jit(solution)/shard_map/ppermute | solution.py:12
  93.8 7.2 %all-to-all-start = ((f32[4,1,2,32,128]{4,3,2,1,0:T(8,128)}), f32[4,1,2,32,128]{4,3,2,1,0:T(8,128)S(1)}, u32[]{:S(2)}, u32[]{:S(2)}) async-start(f32[4,1,2,32,128]{4,3,2,1,0:T(8,128)} %copy.78), calls=%async_computation | async-start | bytes 262144 | tf_op jit(solution)/shard_map/all_to_all | solution.py:22
where the time goes:
time: 102 us
  local copies, waits for them, and re-layouts  52 us (51%)
  other arithmetic  28.5 us (28%)
  starting transfers between devices  17.1 us (17%)
  waiting for transfers between devices  3.55 us (3%)
    sub x4, other arithmetic, advance(): real_part * derivative(imag_part, direction)  15.8 us
    concatenate x14, local copies, waits for them, and re-layouts, derivative(): forward = jnp.roll(values, -1, direction) - jnp.roll(values, 1, direction)  14.9 us
    slice x10, local copies, waits for them, and re-layouts, derivative(): forward = jnp.roll(values, -1, direction) - jnp.roll(values, 1, direction)  14.6 us
    concatenate x8, local copies, waits for them, and re-layouts, derivative(): farther = jnp.roll(values, -2, direction) - jnp.roll(values, 2, direction)  11 us
    ppermute x2, starting transfers between devices, shifted(): return lax.ppermute(block, axis, route)  9.19 us
    all_to_all x2, starting transfers between devices, sum_at_owner(): tiles = lax.all_to_all(cut_along(x, dim, peers), axis, 0, 0, tiled=True)  7.95 us
    while x12, local copies, waits for them, and re-layouts  4.97 us
    all_to_all x2, waiting for transfers between devices, sum_at_owner(): tiles = lax.all_to_all(cut_along(x, dim, peers), axis, 0, 0, tiled=True)  3.55 us
  transfers between devices with their start and end apart: 4, of which 1 were waited for; matrix products, arithmetic and copies ran while one was open for 74% of the time, Pallas kernels for 0%

commit v1 on v0

v1 whole, which is shorter than its diff:
```python
import jax
import jax.numpy as jnp
from jax import lax
from jax.experimental import pallas as pl
from jax.experimental.pallas import tpu as pltpu
from jax.sharding import PartitionSpec as P

MESH = pl.DeviceIdType.MESH
F32 = jnp.float32
BF16 = jnp.bfloat16


def stencil(n, transposed):
    i = lax.broadcasted_iota(jnp.int32, (n, n), 0)
    j = lax.broadcasted_iota(jnp.int32, (n, n), 1)
    d = (i - j if transposed else j - i) + n
    d = jnp.where(d >= n, d - n, d)
    near = jnp.where(d == 1, 8.0, 0.0) - jnp.where(d == n - 1, 8.0, 0.0)
    far = jnp.where(d == n - 2, 1.0, 0.0) - jnp.where(d == 2, 1.0, 0.0)
    return (near + far).astype(BF16)


def make_kernel(rings):
    def kernel(
        orb, occ, out,
        own, outer, inner, below, above, weights, mat_x, mat_y,
        x_acc, x_in, y_acc, pairs, main_out, main_in, extra_out, extra_in,
        load_sem, outer_send, outer_recv, inner_send, inner_recv, down_send, down_recv, up_send, up_recv,
        weight_send, weight_recv, x_send, x_recv, main_send, main_recv, extra_send, extra_recv,
    ):
        bands = own.shape[0]
        b = lax.axis_index("band")
        g = lax.axis_index("grid")
        ring, s = g // 2, g % 2
        yl, c = b // 2, b % 2
        me = s * 4 + b

        def device(r, s_, yl_, c_):
            return {"band": 2 * yl_ + c_, "grid": 2 * ((r + rings) % rings) + s_}

        load = pltpu.make_async_copy(orb, own, load_sem)
        load.start()

        flips = [(1, 0, 0), (1, 0, 1), (0, 1, 0), (1, 1, 0), (0, 1, 1), (1, 1, 1), (0, 0, 1)]
        peers = [((s + i) % 2, (yl + j) % 2, (c + k) % 2) for i, j, k in flips]
        yo = 1 - yl
        barrier = pltpu.get_barrier_semaphore()

        def greet(target):
            pl.semaphore_signal(barrier, inc=1, device_id=target, device_id_type=MESH)

        for s_, yl_, c_ in peers:
            greet(device(ring, s_, yl_, c_))
        greet(device(ring + 1, s, yl, c))
        greet(device(ring - 1, s, yl, c))
        back = ring + 2 * s - 1
        greet(device(back, 0, yo, c))
        greet(device(back, 1, yo, c))

        for n in range(bands):
            weights[b, n : n + 1, :] = jnp.full((1, 128), occ[n], F32)
        mat_x[...] = stencil(128, False)
        mat_y[...] = stencil(128, True)
        x_acc[...] = jnp.zeros_like(x_acc)
        y_acc[...] = jnp.zeros_like(y_acc)
        load.wait()
        pl.semaphore_wait(barrier, 11)

        def send(src, dst, ssem, rsem, target):
            copy = pltpu.make_async_remote_copy(
                src_ref=src, dst_ref=dst, send_sem=ssem, recv_sem=rsem, device_id=target, device_id_type=MESH
            )
            copy.start()
            return copy

        sent = []

        def exchange(plane, slots, ssem, rsem):
            for k, (s_, yl_, c_) in enumerate(peers):
                row = pl.multiple_of(32 * (2 * (1 - yl_) + c_) + 16 * s_, 16)
                sent.append(
                    send(
                        own.at[:, :, plane, pl.ds(row, 16), :], slots.at[me], ssem.at[k], rsem.at[me],
                        device(ring, s_, yl_, c_),
                    )
                )
            row = pl.multiple_of(32 * (2 * yo + c) + 16 * s, 16)
            pltpu.make_async_copy(orb.at[:, :, plane, pl.ds(row, 16), :], slots.at[me], rsem.at[me]).start()

        exchange(s, outer, outer_send, outer_recv)
        for k, (j, i) in enumerate([(0, 1), (1, 0), (1, 1)]):
            sent.append(
                send(
                    weights.at[b], weights.at[b], weight_send.at[k], weight_recv.at[b],
                    device(ring, s, (yl + j) % 2, (c + i) % 2),
                )
            )

        def x_step(n, _):
            w = occ[n]
            for z in range(2):
                re = own[n, 0, z]
                im = own[n, 1, z]
                dre = jnp.dot(mat_x[...], re, preferred_element_type=F32)
                dim = jnp.dot(mat_x[...], im, preferred_element_type=F32)
                x_acc[z] += w * (re.astype(F32) * dim - im.astype(F32) * dre)
            return 0

        lax.fori_loop(0, bands, x_step, 0)

        exchange(1 - s, inner, inner_send, inner_recv)
        for j in range(1, 4):
            to = (b + j) % 4
            sent.append(
                send(
                    x_acc.at[:, pl.ds(pl.multiple_of(32 * to, 32), 32), :], x_in.at[b],
                    x_send.at[j - 1], x_recv.at[b], device(ring, s, to // 2, to % 2),
                )
            )

        def arrived(ref, sem):
            pltpu.make_async_copy(ref, ref, sem).wait()

        for j in range(1, 4):
            q = (b + j) % 4
            arrived(weights.at[q], weight_recv.at[q])

        def y_current(slots, k, q, plane):
            def step(m, total):
                n = 4 * m
                block = slots[k, pl.ds(n, 4)]
                grad = jnp.dot(block.reshape(128, 128), mat_y[...], preferred_element_type=F32).reshape(4, 2, 16, 128)
                for i in range(4):
                    w = weights[q, pl.ds(n + i, 1), :]
                    re = block[i, 0].astype(F32)
                    im = block[i, 1].astype(F32)
                    total = total + w * (re * grad[i, 1] - im * grad[i, 0])
                return total

            y_acc[plane] = lax.fori_loop(0, bands // 4, step, y_acc[plane])

        for j, i in [(0, 0), (0, 1), (1, 0), (1, 1)]:
            q = 2 * ((yl + j) % 2) + (c + i) % 2
            for s_ in range(2):
                k = 4 * s_ + q
                arrived(outer.at[k], outer_recv.at[k])
                if s_ == 0:
                    sent.append(send(outer.at[k], above.at[q], down_send.at[q], down_recv.at[q], device(ring - 1, s, yl, c)))
                else:
                    sent.append(send(outer.at[k], below.at[q], up_send.at[q], up_recv.at[q], device(ring + 1, s, yl, c)))
                y_current(outer, k, q, 3 * s_)

        pairs[...] = jnp.zeros_like(pairs)
        for j, i in [(0, 0), (0, 1), (1, 0), (1, 1)]:
            q = 2 * ((yl + j) % 2) + (c + i) % 2
            arrived(above.at[q], down_recv.at[q])
            arrived(below.at[q], up_recv.at[q])
            arrived(inner.at[q], inner_recv.at[q])
            arrived(inner.at[4 + q], inner_recv.at[4 + q])

            def z_step(n, sums):
                w = weights[q, pl.ds(n, 1), :]

                def field(slots, k):
                    return slots[k, n, 0].astype(F32), slots[k, n, 1].astype(F32)

                def term(u, v):
                    return u[0] * v[1] - u[1] * v[0]

                def weighted(u):
                    return w * u[0], w * u[1]

                a0, b1 = field(outer, q), field(outer, 4 + q)
                a1, b0 = field(inner, q), field(inner, 4 + q)
                nxt, prv = field(above, q), field(below, q)
                wa1, wb0, wn = weighted(a1), weighted(b0), weighted(nxt)
                terms = (
                    term(a0, wa1), term(wa1, b0), term(wb0, b1), term(a0, wb0), term(wa1, b1),
                    term(b1, wn), term(b0, wn), term(prv, wa1),
                )
                return tuple(x + t for x, t in zip(sums, terms))

            sums = lax.fori_loop(0, bands, z_step, tuple(pairs[p] for p in range(8)))
            for p in range(8):
                pairs[p] = sums[p]
            y_current(inner, q, q, 1)
            y_current(inner, 4 + q, q, 2)

        a01, a1b0, b01, a0b0, a1b1, b1n0, b0n0, p1a1 = (pairs[p] for p in range(8))
        near, far = 8.0 / 12.0, 1.0 / 12.0
        extra_out[0] = near * b1n0 - far * b0n0
        extra_out[1] = -far * p1a1
        main_out[0, 0, 0] = near * a01 - far * a0b0
        main_out[0, 0, 1] = near * (a1b0 + a01) - far * (a1b1 + p1a1)
        main_out[1, 0, 0] = near * (b01 + a1b0) - far * (b0n0 + a0b0)
        main_out[1, 0, 1] = near * (b1n0 + b01) - far * a1b1
        for p in range(4):
            main_out[p // 2, 1, p % 2] = y_acc[p] * (1.0 / 12.0)
        for e, r in ((0, ring + 1), (1, ring - 1)):
            sent.append(send(extra_out.at[e], extra_in.at[s], extra_send.at[e], extra_recv.at[s], device(r, e, yo, c)))
        for e in range(2):
            sent.append(send(main_out.at[e], main_in.at[s], main_send.at[e], main_recv.at[s], device(ring, e, yo, c)))

        total = x_acc[:, pl.ds(pl.multiple_of(32 * b, 32), 32), :]
        for j in range(1, 4):
            q = (b + j) % 4
            arrived(x_in.at[q], x_recv.at[q])
            total = total + x_in[q]
        out[1] = total * (1.0 / 12.0)
        for h in range(2):
            rows = slice(16 * h, 16 * h + 16)
            arrived(main_in.at[h], main_recv.at[h])
            arrived(extra_in.at[h], extra_recv.at[h])
            out[0, :, rows, :] = main_in[h, 0]
            out[2, :, rows, :] = main_in[h, 1]
            out[0, s, rows, :] += extra_in[h]
        for copy in sent:
            copy.wait_send()

    return kernel


def solution(mesh):
    rings = mesh.shape["grid"] // 2

    def per_device(orbitals, occupations):
        n = orbitals.shape[0]
        dma = pltpu.SemaphoreType.DMA
        chunk = (n, 2, 16, 128)
        return pl.pallas_call(
            make_kernel(rings),
            out_shape=jax.ShapeDtypeStruct((3, 2, 32, 128), F32),
            in_specs=[pl.BlockSpec(memory_space=pl.ANY), pl.BlockSpec(memory_space=pltpu.SMEM)],
            out_specs=pl.BlockSpec(memory_space=pltpu.VMEM),
            scratch_shapes=[
                pltpu.VMEM((n, 2, 2, 128, 128), BF16),
                pltpu.VMEM((8, *chunk), BF16),
                pltpu.VMEM((8, *chunk), BF16),
                pltpu.VMEM((4, *chunk), BF16),
                pltpu.VMEM((4, *chunk), BF16),
                pltpu.VMEM((4, n, 128), F32),
                pltpu.VMEM((128, 128), BF16),
                pltpu.VMEM((128, 128), BF16),
                pltpu.VMEM((2, 128, 128), F32),
                pltpu.VMEM((4, 2, 32, 128), F32),
                pltpu.VMEM((4, 16, 128), F32),
                pltpu.VMEM((8, 16, 128), F32),
                pltpu.VMEM((2, 2, 2, 16, 128), F32),
                pltpu.VMEM((2, 2, 2, 16, 128), F32),
                pltpu.VMEM((2, 16, 128), F32),
                pltpu.VMEM((2, 16, 128), F32),
                dma,
                dma((7,)), dma((8,)),
                dma((7,)), dma((8,)),
                dma((4,)), dma((4,)),
                dma((4,)), dma((4,)),
                dma((3,)), dma((4,)),
                dma((3,)), dma((4,)),
                dma((2,)), dma((2,)),
                dma((2,)), dma((2,)),
            ],
            compiler_params=pltpu.CompilerParams(collective_id=0, has_side_effects=True),
        )(orbitals, occupations)

    return jax.shard_map(
        per_device,
        mesh=mesh,
        in_specs=(P("band", None, "grid", None, None), P("band")),
        out_specs=P(None, "grid", "band", None),
        check_vma=False,
    )
```

time: 102 us -> 47.9 us (0.47)
  local copies, waits for them, and re-layouts: 52 us -> 1.54 us
  Pallas kernels: 0 us -> 45.9 us
  other arithmetic: 28.5 us -> 0 us
  starting transfers between devices: 17.1 us -> 0 us
  waiting for transfers between devices: 3.55 us -> 0 us
    pallas_call x0 -> x1, Pallas kernels: none -> 45.9 us  [per_device(): pl.pallas_call(make_kernel(rings), out_shape=jax.ShapeDtypeStruct((3, 2,...]
    concatenate x22 -> x0, local copies, waits for them, and re-layouts: 25.9 us -> none  [the longest x14 14.9 us: derivative(): forward = jnp.roll(values, -1, direction) - jnp.roll(values, 1, direction)]
    sub x4 -> x0, other arithmetic: 15.8 us -> none  [advance(): real_part * derivative(imag_part, direction)]
    slice x10 -> x0, local copies, waits for them, and re-layouts: 14.6 us -> none  [derivative(): forward = jnp.roll(values, -1, direction) - jnp.roll(values, 1, direction)]
    ppermute x2 -> x0, starting transfers between devices: 9.19 us -> none  [shifted(): return lax.ppermute(block, axis, route)]
    all_to_all x2 -> x0, starting transfers between devices: 7.95 us -> none  [sum_at_owner(): tiles = lax.all_to_all(cut_along(x, dim, peers), axis, 0, 0, tiled=True)]
    convert_element_type x6 -> x0, other arithmetic: 5.91 us -> none  [the longest x1 2.1 us: depth_part(): lower_rim = shifted(orbitals, 'grid', 1).astype(jnp.float32)]
    while x12 -> x0, local copies, waits for them, and re-layouts: 4.97 us -> none
  transfers between devices with their start and end apart: 4 -> 0, of which waited for: 1 -> 0; matrix products, arithmetic and copies ran while one was open for 74% -> 0% of each run, Pallas kernels for 0% -> 0%
where the time goes in v1:
time: 47.9 us; the launch traced here: 47.4 us
  Pallas kernels  45.9 us (96%)
  local copies, waits for them, and re-layouts  1.54 us (3%)
    pallas_call x1, Pallas kernels, per_device(): pl.pallas_call(make_kernel(rings), out_shape=jax.ShapeDtypeStruct((3, 2,...  45.9 us
    unnamed x1, local copies, waits for them, and re-layouts  1.54 us

profile of v1, /device:TPU:1, one launch (start us, length us, event | category | flops | bytes accessed | tf_op | source)
XLA Modules:
  0.0 47.4 jit_solution(12627287482256090447)
XLA Ops:
  0.0 45.9 %shard_map.28 = f32[3,2,32,128]{3,2,1,0:T(8,128)} custom-call(bf16[16,2,2,128,128]{4,3,2,1,0:T(8,128)(2,1)} %orb.1, f32[16]{0:T(128)} %occ.1), custom_call_target="tpu_custom_call" | custom-call | tf_op jit(solution)/shard_map/pallas_call | solution.py:230
  45.9 1.5 %copy.4 = f32[3,2,32,128]{3,2,1,0:T(8,128)} copy(f32[3,2,32,128]{3,2,1,0:T(8,128)} %shard_map.28) | data formatting | bytes 196608

commit v2 on v1

--- a/solution.py
+++ b/solution.py
@@ -22,10 +22,10 @@
 
 def make_kernel(rings):
     def kernel(
-        orb, occ, out,
-        own, outer, inner, below, above, weights, mat_x, mat_y,
+        orb, occ_in, out,
+        occ, own, outer, inner, below, above, weights, mat_x, mat_y,
         x_acc, x_in, y_acc, pairs, main_out, main_in, extra_out, extra_in,
-        load_sem, outer_send, outer_recv, inner_send, inner_recv, down_send, down_recv, up_send, up_recv,
+        occ_sem, load_sem, outer_send, outer_recv, inner_send, inner_recv, down_send, down_recv, up_send, up_recv,
         weight_send, weight_recv, x_send, x_recv, main_send, main_recv, extra_send, extra_recv,
     ):
         bands = own.shape[0]
@@ -38,10 +38,7 @@
         def device(r, s_, yl_, c_):
             return {"band": 2 * yl_ + c_, "grid": 2 * ((r + rings) % rings) + s_}
 
-        load = pltpu.make_async_copy(orb, own, load_sem)
-        load.start()
-
-        flips = [(1, 0, 0), (1, 0, 1), (0, 1, 0), (1, 1, 0), (0, 1, 1), (1, 1, 1), (0, 0, 1)]
+        flips = [(0, 0, 1), (1, 0, 0), (1, 0, 1), (0, 1, 0), (1, 1, 0), (0, 1, 1), (1, 1, 1)]
         peers = [((s + i) % 2, (yl + j) % 2, (c + k) % 2) for i, j, k in flips]
         yo = 1 - yl
         barrier = pltpu.get_barrier_semaphore()
@@ -57,13 +54,27 @@
         greet(device(back, 0, yo, c))
         greet(device(back, 1, yo, c))
 
-        for n in range(bands):
-            weights[b, n : n + 1, :] = jnp.full((1, 128), occ[n], F32)
+        occ_load = pltpu.make_async_copy(occ_in, occ, occ_sem)
+        occ_load.start()
+        loads = [
+            pltpu.make_async_copy(orb.at[:, :, plane], own.at[:, :, plane], load_sem.at[k])
+            for k, plane in enumerate((s, 1 - s))
+        ]
+        for load in loads:
+            load.start()
+        my_row = pl.multiple_of(32 * (2 * yo + c) + 16 * s, 16)
+        for plane, slots, sem in ((s, outer, outer_recv), (1 - s, inner, inner_recv)):
+            pltpu.make_async_copy(orb.at[:, :, plane, pl.ds(my_row, 16), :], slots.at[me], sem.at[me]).start()
         mat_x[...] = stencil(128, False)
         mat_y[...] = stencil(128, True)
         x_acc[...] = jnp.zeros_like(x_acc)
         y_acc[...] = jnp.zeros_like(y_acc)
-        load.wait()
+        pairs[...] = jnp.zeros_like(pairs)
+
+        occ_load.wait()
+        for n in range(bands):
+            weights[b, n : n + 1, :] = jnp.full((1, 128), occ[n], F32)
+        loads[0].wait()
         pl.semaphore_wait(barrier, 11)
 
         def send(src, dst, ssem, rsem, target):
@@ -84,10 +95,7 @@
                         device(ring, s_, yl_, c_),
                     )
                 )
-            row = pl.multiple_of(32 * (2 * yo + c) + 16 * s, 16)
-            pltpu.make_async_copy(orb.at[:, :, plane, pl.ds(row, 16), :], slots.at[me], rsem.at[me]).start()
-
-        exchange(s, outer, outer_send, outer_recv)
+
         for k, (j, i) in enumerate([(0, 1), (1, 0), (1, 1)]):
             sent.append(
                 send(
@@ -95,6 +103,9 @@
                     device(ring, s, (yl + j) % 2, (c + i) % 2),
                 )
             )
+
+        exchange(s, outer, outer_send, outer_recv)
+        loads[1].wait()
 
         def x_step(n, _):
             w = occ[n]
@@ -121,23 +132,15 @@
         def arrived(ref, sem):
             pltpu.make_async_copy(ref, ref, sem).wait()
 
-        for j in range(1, 4):
-            q = (b + j) % 4
-            arrived(weights.at[q], weight_recv.at[q])
-
         def y_current(slots, k, q, plane):
-            def step(m, total):
-                n = 4 * m
-                block = slots[k, pl.ds(n, 4)]
-                grad = jnp.dot(block.reshape(128, 128), mat_y[...], preferred_element_type=F32).reshape(4, 2, 16, 128)
-                for i in range(4):
-                    w = weights[q, pl.ds(n + i, 1), :]
-                    re = block[i, 0].astype(F32)
-                    im = block[i, 1].astype(F32)
-                    total = total + w * (re * grad[i, 1] - im * grad[i, 0])
-                return total
-
-            y_acc[plane] = lax.fori_loop(0, bands // 4, step, y_acc[plane])
+            block = slots[k]
+            grad = jnp.dot(block.reshape(bands * 32, 128), mat_y[...], preferred_element_type=F32)
+            total = y_acc[plane]
+            for n in range(bands):
+                re, im = block[n, 0].astype(F32), block[n, 1].astype(F32)
+                dre, dim = grad[32 * n : 32 * n + 16], grad[32 * n + 16 : 32 * n + 32]
+                total = total + weights[q, n : n + 1, :] * (re * dim - im * dre)
+            y_acc[plane] = total
 
         for j, i in [(0, 0), (0, 1), (1, 0), (1, 1)]:
             q = 2 * ((yl + j) % 2) + (c + i) % 2
@@ -148,9 +151,12 @@
                     sent.append(send(outer.at[k], above.at[q], down_send.at[q], down_recv.at[q], device(ring - 1, s, yl, c)))
                 else:
                     sent.append(send(outer.at[k], below.at[q], up_send.at[q], up_recv.at[q], device(ring + 1, s, yl, c)))
+            if j + i > 0:
+                arrived(weights.at[q], weight_recv.at[q])
+            for s_ in range(2):
+                k = 4 * s_ + q
                 y_current(outer, k, q, 3 * s_)
 
-        pairs[...] = jnp.zeros_like(pairs)
         for j, i in [(0, 0), (0, 1), (1, 0), (1, 1)]:
             q = 2 * ((yl + j) % 2) + (c + i) % 2
             arrived(above.at[q], down_recv.at[q])
@@ -230,9 +236,10 @@
         return pl.pallas_call(
             make_kernel(rings),
             out_shape=jax.ShapeDtypeStruct((3, 2, 32, 128), F32),
-            in_specs=[pl.BlockSpec(memory_space=pl.ANY), pl.BlockSpec(memory_space=pltpu.SMEM)],
+            in_specs=[pl.BlockSpec(memory_space=pl.ANY), pl.BlockSpec(memory_space=pl.ANY)],
             out_specs=pl.BlockSpec(memory_space=pltpu.VMEM),
             scratch_shapes=[
+                pltpu.SMEM((n,), F32),
                 pltpu.VMEM((n, 2, 2, 128, 128), BF16),
                 pltpu.VMEM((8, *chunk), BF16),
                 pltpu.VMEM((8, *chunk), BF16),
@@ -250,6 +257,7 @@
                 pltpu.VMEM((2, 16, 128), F32),
                 pltpu.VMEM((2, 16, 128), F32),
                 dma,
+                dma((2,)),
                 dma((7,)), dma((8,)),
                 dma((7,)), dma((8,)),
                 dma((4,)), dma((4,)),

time: 47.9 us -> 40.8 us (0.85)
  Pallas kernels: 45.9 us -> 39.1 us
    pallas_call x1, Pallas kernels: 45.9 us -> 39.1 us  [per_device(): pl.pallas_call(make_kernel(rings), out_shape=jax.ShapeDtypeStruct((3, 2,...]
where the time goes in v2:
time: 40.8 us; the launch traced here: 40.7 us
  Pallas kernels  39.1 us (96%)
  local copies, waits for them, and re-layouts  1.54 us (4%)
    pallas_call x1, Pallas kernels, per_device(): pl.pallas_call(make_kernel(rings), out_shape=jax.ShapeDtypeStruct((3, 2,...  39.1 us
    unnamed x1, local copies, waits for them, and re-layouts  1.54 us

profile of v2, /device:TPU:1, one launch (start us, length us, event | category | flops | bytes accessed | tf_op | source)
XLA Modules:
  0.0 40.7 jit_solution(5049415865855213441)
XLA Ops:
  0.0 39.1 %shard_map.28 = f32[3,2,32,128]{3,2,1,0:T(8,128)} custom-call(bf16[16,2,2,128,128]{4,3,2,1,0:T(8,128)(2,1)} %orb.1, f32[16]{0:T(128)} %occ_in.1), custom_call_target="tpu_custom_call" | custom-call | tf_op jit(solution)/shard_map/pallas_call | solution.py:236
  39.1 1.5 %copy.4 = f32[3,2,32,128]{3,2,1,0:T(8,128)} copy(f32[3,2,32,128]{3,2,1,0:T(8,128)} %shard_map.28) | data formatting | bytes 196608

commit v3 on v2

--- a/solution.py
+++ b/solution.py
@@ -235,7 +235,7 @@
         chunk = (n, 2, 16, 128)
         return pl.pallas_call(
             make_kernel(rings),
-            out_shape=jax.ShapeDtypeStruct((3, 2, 32, 128), F32),
+            out_shape=pltpu.VMEM((3, 2, 32, 128), F32),
             in_specs=[pl.BlockSpec(memory_space=pl.ANY), pl.BlockSpec(memory_space=pl.ANY)],
             out_specs=pl.BlockSpec(memory_space=pltpu.VMEM),
             scratch_shapes=[

time: 40.8 us -> 39.3 us (0.963)
  local copies, waits for them, and re-layouts: 1.54 us -> 0.64 us
  Pallas kernels: 39.1 us -> 38.5 us
    unnamed x1, local copies, waits for them, and re-layouts: 1.54 us -> 0.64 us
    pallas_call x1, Pallas kernels: 39.1 us -> 38.5 us  [per_device(): pl.pallas_call(make_kernel(rings), out_shape=pltpu.VMEM((3, 2, 32, 128),...]
where the time goes in v3:
time: 39.3 us; the launch traced here: 39.2 us
  Pallas kernels  38.5 us (98%)
  local copies, waits for them, and re-layouts  0.64 us (2%)
    pallas_call x1, Pallas kernels, per_device(): pl.pallas_call(make_kernel(rings), out_shape=pltpu.VMEM((3, 2, 32, 128),...  38.5 us

profile of v3, /device:TPU:1, one launch (start us, length us, event | category | flops | bytes accessed | tf_op | source)
XLA Modules:
  0.0 39.2 jit_solution(5160630589681974859)
XLA Ops:
  0.0 38.5 %shard_map.28 = f32[3,2,32,128]{3,2,1,0:T(8,128)S(1)} custom-call(bf16[16,2,2,128,128]{4,3,2,1,0:T(8,128)(2,1)} %orb.1, f32[16]{0:T(128)} %occ_in.1), custom_call_target="tpu_custom_call" | custom-call | tf_op jit(solution)/shard_map/pallas_call | solution.py:236
  38.5 0.6 %copy.4 = f32[3,2,32,128]{3,2,1,0:T(8,128)} copy(f32[3,2,32,128]{3,2,1,0:T(8,128)S(1)} %shard_map.28) | data formatting | bytes 196608

commit v4 on v3

v4 whole, which is shorter than its diff:
```python
import jax
import jax.numpy as jnp
from jax import lax
from jax.experimental import pallas as pl
from jax.experimental.pallas import tpu as pltpu
from jax.sharding import PartitionSpec as P

MESH = pl.DeviceIdType.MESH
F32 = jnp.float32
BF16 = jnp.bfloat16


def stencil(n, transposed):
    i = lax.broadcasted_iota(jnp.int32, (n, n), 0)
    j = lax.broadcasted_iota(jnp.int32, (n, n), 1)
    d = (i - j if transposed else j - i) + n
    d = jnp.where(d >= n, d - n, d)
    near = jnp.where(d == 1, 8.0, 0.0) - jnp.where(d == n - 1, 8.0, 0.0)
    far = jnp.where(d == n - 2, 1.0, 0.0) - jnp.where(d == 2, 1.0, 0.0)
    return (near + far).astype(BF16)


def make_kernel(rings):
    def kernel(
        orb, occ_in, out,
        occ, own, outer, late, weights, mat_x, mat_y,
        x_acc, x_in, y_acc, pairs, main_out, main_in, extra_out, extra_in,
        occ_sem, load_sem, send_sem, outer_sem, late_sem, weight_sem, x_sem, main_sem, extra_sem, up_ready, down_ready,
    ):
        bands = own.shape[0]
        b = lax.axis_index("band")
        g = lax.axis_index("grid")
        ring, s = g // 2, g % 2
        yl, c = b // 2, b % 2
        yo, co = 1 - yl, 1 - c
        turn = ring % 4

        def device(r, s_, yl_, c_):
            return {"band": 2 * yl_ + c_, "grid": 2 * ((r + rings) % rings) + s_}

        flips = [(0, 0, 1), (1, 0, 0), (1, 0, 1), (0, 1, 0), (1, 1, 0), (0, 1, 1), (1, 1, 1)]
        peers = [((s + i) % 2, (yl + j) % 2, (c + k) % 2) for i, j, k in flips]
        above, below = device(ring + 1, s, yl, c), device(ring - 1, s, yl, c)
        barrier = pltpu.get_barrier_semaphore()

        def signal(sem, target):
            pl.semaphore_signal(sem, inc=1, device_id=target, device_id_type=MESH)

        for s_, yl_, c_ in peers:
            signal(barrier, device(ring, s_, yl_, c_))
        pl.when(turn != 3)(lambda: signal(barrier, above))
        pl.when(turn == 0)(lambda: signal(barrier, below))

        occ_load = pltpu.make_async_copy(occ_in, occ, occ_sem)
        loads = [
            pltpu.make_async_copy(orb.at[:, :, plane], own.at[:, :, plane], load_sem.at[k])
            for k, plane in enumerate((s, 1 - s))
        ]
        loads[0].start()
        occ_load.start()
        loads[1].start()

        def my_rows(s_, yl_, c_):
            return pl.ds(pl.multiple_of(32 * (2 * (1 - yl_) + 1 - c_) + 16 * s_, 16), 16)

        mine = my_rows(s, yl, c)
        pltpu.make_async_copy(orb.at[:, :, s, mine, :], outer.at[b, s], outer_sem.at[b]).start()
        pltpu.make_async_copy(orb.at[:, :, 1 - s, mine, :], late.at[b, s], late_sem.at[b]).start()
        mat_x[...] = stencil(128, False)
        mat_y[...] = stencil(128, True)
        x_acc[...] = jnp.zeros_like(x_acc)
        y_acc[...] = jnp.zeros_like(y_acc)
        pairs[...] = jnp.zeros_like(pairs)
        occ_load.wait()
        for n in range(bands):
            weights[b, n : n + 1, :] = jnp.full((1, 128), occ[n], F32)
        loads[0].wait()
        pl.semaphore_wait(barrier, 7 + (turn + 1) // 2)

        sent = []

        def send(src, dst, sem, target):
            copy = pltpu.make_async_remote_copy(
                src_ref=src, dst_ref=dst, send_sem=send_sem, recv_sem=sem, device_id=target, device_id_type=MESH
            )
            copy.start()
            sent.append(copy)

        def arrived(ref, sem):
            pltpu.make_async_copy(ref, ref, sem).wait()

        for j, i in [(0, 1), (1, 0), (1, 1)]:
            send(weights.at[b], weights.at[b], weight_sem, device(ring, s, (yl + j) % 2, (c + i) % 2))
        for s_, yl_, c_ in peers:
            send(own.at[:, :, s, my_rows(s_, yl_, c_), :], outer.at[b, s], outer_sem.at[b], device(ring, s_, yl_, c_))
        pl.when(turn != 0)(lambda: signal(up_ready, below))
        pl.when(turn == 3)(lambda: signal(down_ready, above))
        loads[1].wait()

        def x_step(n, _):
            w = occ[n]
            for z in range(2):
                re = own[n, 0, z]
                im = own[n, 1, z]
                dre = jnp.dot(mat_x[...], re, preferred_element_type=F32)
                dim = jnp.dot(mat_x[...], im, preferred_element_type=F32)
                x_acc[z] += w * (re.astype(F32) * dim - im.astype(F32) * dre)
            return 0

        lax.fori_loop(0, bands, x_step, 0)

        for s_, yl_, c_ in peers:
            send(own.at[:, :, 1 - s, my_rows(s_, yl_, c_), :], late.at[b, s], late_sem.at[b], device(ring, s_, yl_, c_))
        for j in range(1, 4):
            to = (b + j) % 4
            rows = pl.ds(pl.multiple_of(32 * to, 32), 32)
            send(x_acc.at[:, rows, :], x_in.at[b], x_sem, device(ring, s, to // 2, to % 2))

        arrived(weights.at[pl.ds(0, 3)], weight_sem)
        pl.when(turn != 3)(lambda: pl.semaphore_wait(up_ready, 1))
        pl.when(turn == 0)(lambda: pl.semaphore_wait(down_ready, 1))

        def y_current(slots, q, k, plane):
            block = slots[q, k]
            grad = jnp.dot(block.reshape(bands * 32, 128), mat_y[...], preferred_element_type=F32)
            total = y_acc[plane]
            for n in range(bands):
                re, im = block[n, 0].astype(F32), block[n, 1].astype(F32)
                dre, dim = grad[32 * n : 32 * n + 16], grad[32 * n + 16 : 32 * n + 32]
                total = total + weights[q, n : n + 1, :] * (re * dim - im * dre)
            y_acc[plane] = total

        order = [2 * ((yl + j) % 2) + (c + i) % 2 for j, i in [(0, 0), (0, 1), (1, 0), (1, 1)]]

        for q in order:
            arrived(outer.at[q], outer_sem.at[q])
            send(outer.at[q, 0], late.at[q, 2], late_sem.at[q], below)
            send(outer.at[q, 1], late.at[q, 3], late_sem.at[q], above)
            y_current(outer, q, 0, 0)
            y_current(outer, q, 1, 3)

        def to_owner(e, part, size):
            send(main_out.at[e, pl.ds(part, size)], main_in.at[s, pl.ds(part, size)], main_sem, device(ring, e, yo, co))

        near, far = 8.0 / 12.0, 1.0 / 12.0
        for e in range(2):
            main_out[e, 2] = far * y_acc[3 * e]
            to_owner(e, 2, 1)

        def pair_sums(q, picked):
            def z_step(n, sums):
                w = weights[q, pl.ds(n, 1), :]

                def field(slots, k):
                    return slots[q, k, n, 0].astype(F32), slots[q, k, n, 1].astype(F32)

                def term(u, v):
                    return u[0] * v[1] - u[1] * v[0]

                def weighted(u):
                    return w * u[0], w * u[1]

                a0, b1 = field(outer, 0), field(outer, 1)
                a1, b0, nxt, prv = field(late, 0), field(late, 1), field(late, 2), field(late, 3)
                wa1, wb0, wn = weighted(a1), weighted(b0), weighted(nxt)
                terms = [
                    (b1, wn), (b0, wn), (prv, wa1), (a0, wa1), (wa1, b0), (wb0, b1), (a0, wb0), (wa1, b1),
                ]
                return tuple(x + term(*terms[p]) for x, p in zip(sums, picked))

            sums = lax.fori_loop(0, bands, z_step, tuple(pairs[p] for p in picked), unroll=4)
            for p, x in zip(picked, sums):
                pairs[p] = x

        for q in order[:3]:
            arrived(late.at[q], late_sem.at[q])
            pair_sums(q, range(8))
            y_current(late, q, 0, 1)
            y_current(late, q, 1, 2)
        q = order[3]
        arrived(late.at[q], late_sem.at[q])
        pair_sums(q, range(3))
        b1n0, b0n0, p1a1 = (pairs[p] for p in range(3))
        extra_out[0] = near * b1n0 - far * b0n0
        extra_out[1] = -far * p1a1
        for e, r in ((0, ring + 1), (1, ring - 1)):
            send(extra_out.at[e], extra_in.at[s], extra_sem, device(r, e, yo, co))
        pair_sums(q, range(3, 8))
        a01, a1b0, b01, a0b0, a1b1 = (pairs[p] for p in range(3, 8))
        main_out[0, 0] = near * a01 - far * a0b0
        main_out[0, 1] = near * (a1b0 + a01) - far * (a1b1 + p1a1)
        main_out[1, 0] = near * (b01 + a1b0) - far * (b0n0 + a0b0)
        main_out[1, 1] = near * (b1n0 + b01) - far * a1b1
        for e in range(2):
            to_owner(e, 0, 2)
        y_current(late, q, 0, 1)
        y_current(late, q, 1, 2)
        for e in range(2):
            main_out[e, 3] = far * y_acc[1 + e]
            to_owner(e, 3, 1)

        arrived(x_in.at[pl.ds(0, 3)], x_sem)
        total = x_acc[:, pl.ds(pl.multiple_of(32 * b, 32), 32), :]
        for j in range(1, 4):
            total = total + x_in[(b + j) % 4]
        out[1] = total * far
        arrived(main_in, main_sem)
        arrived(extra_in, extra_sem)
        for h in range(2):
            rows = slice(16 * h, 16 * h + 16)
            out[0, :, rows, :] = main_in[h, :2]
            out[2, s, rows, :] = main_in[h, 2]
            out[2, 1 - s, rows, :] = main_in[h, 3]
            out[0, s, rows, :] += extra_in[h]
        for copy in sent:
            copy.wait_send()

    return kernel


def solution(mesh):
    rings = mesh.shape["grid"] // 2

    def per_device(orbitals, occupations):
        n = orbitals.shape[0]
        dma = pltpu.SemaphoreType.DMA
        chunk = (n, 2, 16, 128)
        return pl.pallas_call(
            make_kernel(rings),
            out_shape=pltpu.VMEM((3, 2, 32, 128), F32),
            in_specs=[pl.BlockSpec(memory_space=pl.ANY), pl.BlockSpec(memory_space=pl.ANY)],
            out_specs=pl.BlockSpec(memory_space=pltpu.VMEM),
            scratch_shapes=[
                pltpu.SMEM((n,), F32),
                pltpu.VMEM((n, 2, 2, 128, 128), BF16),
                pltpu.VMEM((4, 2, *chunk), BF16),
                pltpu.VMEM((4, 4, *chunk), BF16),
                pltpu.VMEM((4, n, 128), F32),
                pltpu.VMEM((128, 128), BF16),
                pltpu.VMEM((128, 128), BF16),
                pltpu.VMEM((2, 128, 128), F32),
                pltpu.VMEM((4, 2, 32, 128), F32),
                pltpu.VMEM((4, 16, 128), F32),
                pltpu.VMEM((8, 16, 128), F32),
                pltpu.VMEM((2, 4, 16, 128), F32),
                pltpu.VMEM((2, 4, 16, 128), F32),
                pltpu.VMEM((2, 16, 128), F32),
                pltpu.VMEM((2, 16, 128), F32),
                dma, dma((2,)), dma, dma((4,)), dma((4,)), dma, dma, dma, dma,
                pltpu.SemaphoreType.REGULAR, pltpu.SemaphoreType.REGULAR,
            ],
            compiler_params=pltpu.CompilerParams(collective_id=0, has_side_effects=True),
        )(orbitals, occupations)

    return jax.shard_map(
        per_device,
        mesh=mesh,
        in_specs=(P("band", None, "grid", None, None), P("band")),
        out_specs=P(None, "grid", "band", None),
        check_vma=False,
    )
```

time: 39.3 us -> 38.9 us (0.990)
  Pallas kernels: 38.5 us -> 38.1 us
    pallas_call x1, Pallas kernels: 38.5 us -> 38.1 us  [per_device(): pl.pallas_call(make_kernel(rings), out_shape=pltpu.VMEM((3, 2, 32, 128),...]
where the time goes in v4:
time: 38.9 us; the launch traced here: 38.7 us
  Pallas kernels  38.1 us (98%)
  local copies, waits for them, and re-layouts  0.64 us (2%)
    pallas_call x1, Pallas kernels, per_device(): pl.pallas_call(make_kernel(rings), out_shape=pltpu.VMEM((3, 2, 32, 128),...  38.1 us

profile of v4, /device:TPU:1, one launch (start us, length us, event | category | flops | bytes accessed | tf_op | source)
XLA Modules:
  0.0 38.7 jit_solution(15416313404392980905)
XLA Ops:
  0.0 38.1 %shard_map.28 = f32[3,2,32,128]{3,2,1,0:T(8,128)S(1)} custom-call(bf16[16,2,2,128,128]{4,3,2,1,0:T(8,128)(2,1)} %orb.1, f32[16]{0:T(128)} %occ_in.1), custom_call_target="tpu_custom_call" | custom-call | tf_op jit(solution)/shard_map/pallas_call | solution.py:228
  38.1 0.6 %copy.4 = f32[3,2,32,128]{3,2,1,0:T(8,128)} copy(f32[3,2,32,128]{3,2,1,0:T(8,128)S(1)} %shard_map.28) | data formatting | bytes 196608

commit v5 on v4

--- a/solution.py
+++ b/solution.py
@@ -20,12 +20,20 @@
     return (near + far).astype(BF16)
 
 
+INNER = [(0, 0, 1), (1, 0, 0), (1, 0, 1), (0, 1, 0), (1, 1, 0), (0, 1, 1), (1, 1, 1)]
+
+
+def EARLY(ring, rings):
+    return ring == 0, ring == rings - 1
+
+
 def make_kernel(rings):
     def kernel(
         orb, occ_in, out,
         occ, own, outer, late, weights, mat_x, mat_y,
-        x_acc, x_in, y_acc, pairs, main_out, main_in, extra_out, extra_in,
-        occ_sem, load_sem, send_sem, outer_sem, late_sem, weight_sem, x_sem, main_sem, extra_sem, up_ready, down_ready,
+        x_acc, x_in, y_acc, pairs, main_out, main_in, extra_out, extra_in, tip_in, relay_in, tip_sums,
+        occ_sem, load_sem, send_sem, outer_sem, edge_sem, same_sem, cross_sem, weight_sem, x_sem, main_sem, extra_sem, tip_sem, relay_sem, sums_sem,
+        up_ready, down_ready,
     ):
         bands = own.shape[0]
         b = lax.axis_index("band")
@@ -50,6 +58,8 @@
             signal(barrier, device(ring, s_, yl_, c_))
         pl.when(turn != 3)(lambda: signal(barrier, above))
         pl.when(turn == 0)(lambda: signal(barrier, below))
+        early, ahead = EARLY(ring, rings)
+        tip_turn, relay_turn = ahead & (s == 1), early & (s == 1)
 
         occ_load = pltpu.make_async_copy(occ_in, occ, occ_sem)
         loads = [
@@ -65,7 +75,7 @@
 
         mine = my_rows(s, yl, c)
         pltpu.make_async_copy(orb.at[:, :, s, mine, :], outer.at[b, s], outer_sem.at[b]).start()
-        pltpu.make_async_copy(orb.at[:, :, 1 - s, mine, :], late.at[b, s], late_sem.at[b]).start()
+        pltpu.make_async_copy(orb.at[:, :, 1 - s, mine, :], late.at[b, s], same_sem.at[b]).start()
         mat_x[...] = stencil(128, False)
         mat_y[...] = stencil(128, True)
         x_acc[...] = jnp.zeros_like(x_acc)
@@ -77,25 +87,43 @@
         loads[0].wait()
         pl.semaphore_wait(barrier, 7 + (turn + 1) // 2)
 
-        sent = []
-
-        def send(src, dst, sem, target):
+        def start(src, dst, sem, target):
             copy = pltpu.make_async_remote_copy(
                 src_ref=src, dst_ref=dst, send_sem=send_sem, recv_sem=sem, device_id=target, device_id_type=MESH
             )
             copy.start()
-            sent.append(copy)
+            return copy
+
+        sent = []
+
+        def send(*args):
+            sent.append(start(*args))
 
         def arrived(ref, sem):
             pltpu.make_async_copy(ref, ref, sem).wait()
 
         for j, i in [(0, 1), (1, 0), (1, 1)]:
             send(weights.at[b], weights.at[b], weight_sem, device(ring, s, (yl + j) % 2, (c + i) % 2))
+        def tip_copy(e):
+            return (own.at[:, :, 0, my_rows(e, yo, co), :], relay_in.at[e], relay_sem, above)
+
+        def sums_copy():
+            return (extra_out.at[2], tip_sums.at[s], sums_sem, device(ring, 0, yo, co))
+
+        def relay_copy(e):
+            return (relay_in.at[e], tip_in, tip_sem, device(ring, e, yo, co))
+
+        @pl.when(tip_turn)
+        def _():
+            loads[1].wait()
+            for e in range(2):
+                start(*tip_copy(e))
+
         for s_, yl_, c_ in peers:
             send(own.at[:, :, s, my_rows(s_, yl_, c_), :], outer.at[b, s], outer_sem.at[b], device(ring, s_, yl_, c_))
         pl.when(turn != 0)(lambda: signal(up_ready, below))
         pl.when(turn == 3)(lambda: signal(down_ready, above))
-        loads[1].wait()
+        pl.when(jnp.logical_not(tip_turn))(lambda: loads[1].wait())
 
         def x_step(n, _):
             w = occ[n]
@@ -109,16 +137,18 @@
 
         lax.fori_loop(0, bands, x_step, 0)
 
-        for s_, yl_, c_ in peers:
-            send(own.at[:, :, 1 - s, my_rows(s_, yl_, c_), :], late.at[b, s], late_sem.at[b], device(ring, s_, yl_, c_))
+        pl.when(turn != 3)(lambda: pl.semaphore_wait(up_ready, 1))
+        pl.when(turn == 0)(lambda: pl.semaphore_wait(down_ready, 1))
+        for i, j, k in INNER:
+            s_, yl_, c_ = (s + i) % 2, (yl + j) % 2, (c + k) % 2
+            sem = (cross_sem if i else same_sem).at[b]
+            send(own.at[:, :, 1 - s, my_rows(s_, yl_, c_), :], late.at[b, s], sem, device(ring, s_, yl_, c_))
         for j in range(1, 4):
             to = (b + j) % 4
             rows = pl.ds(pl.multiple_of(32 * to, 32), 32)
             send(x_acc.at[:, rows, :], x_in.at[b], x_sem, device(ring, s, to // 2, to % 2))
 
         arrived(weights.at[pl.ds(0, 3)], weight_sem)
-        pl.when(turn != 3)(lambda: pl.semaphore_wait(up_ready, 1))
-        pl.when(turn == 0)(lambda: pl.semaphore_wait(down_ready, 1))
 
         def y_current(slots, q, k, plane):
             block = slots[q, k]
@@ -134,8 +164,8 @@
 
         for q in order:
             arrived(outer.at[q], outer_sem.at[q])
-            send(outer.at[q, 0], late.at[q, 2], late_sem.at[q], below)
-            send(outer.at[q, 1], late.at[q, 3], late_sem.at[q], above)
+            send(outer.at[q, 0], late.at[q, 2], edge_sem.at[q], below)
+            send(outer.at[q, 1], late.at[q, 3], edge_sem.at[q], above)
             y_current(outer, q, 0, 0)
             y_current(outer, q, 1, 3)
 
@@ -147,46 +177,63 @@
             main_out[e, 2] = far * y_acc[3 * e]
             to_owner(e, 2, 1)
 
+        def term(u, v):
+            return u[0] * v[1] - u[1] * v[0]
+
+        names = [
+            ("b1", "nxt"), ("b0", "nxt"), ("a1", "prv"), ("a1", "a0"), ("a1", "b0"), ("b0", "b1"), ("b0", "a0"), ("a1", "b1"),
+        ]
+        places = {"a0": (outer, 0), "b1": (outer, 1), "a1": (late, 0), "b0": (late, 1), "nxt": (late, 2), "prv": (late, 3)}
+
         def pair_sums(q, picked):
             def z_step(n, sums):
                 w = weights[q, pl.ds(n, 1), :]
-
-                def field(slots, k):
-                    return slots[q, k, n, 0].astype(F32), slots[q, k, n, 1].astype(F32)
-
-                def term(u, v):
-                    return u[0] * v[1] - u[1] * v[0]
-
-                def weighted(u):
-                    return w * u[0], w * u[1]
-
-                a0, b1 = field(outer, 0), field(outer, 1)
-                a1, b0, nxt, prv = field(late, 0), field(late, 1), field(late, 2), field(late, 3)
-                wa1, wb0, wn = weighted(a1), weighted(b0), weighted(nxt)
-                terms = [
-                    (b1, wn), (b0, wn), (prv, wa1), (a0, wa1), (wa1, b0), (wb0, b1), (a0, wb0), (wa1, b1),
-                ]
-                return tuple(x + term(*terms[p]) for x, p in zip(sums, picked))
+                used = sorted({name for p in picked for name in names[p]})
+                field = {}
+                for name in used:
+                    slots, k = places[name]
+                    field[name] = (slots[q, k, n, 0].astype(F32), slots[q, k, n, 1].astype(F32))
+                scaled = {name: (w * field[name][0], w * field[name][1]) for name in sorted({names[p][0] for p in picked})}
+                return tuple(x + term(scaled[names[p][0]], field[names[p][1]]) for x, p in zip(sums, picked))
 
             sums = lax.fori_loop(0, bands, z_step, tuple(pairs[p] for p in picked), unroll=4)
             for p, x in zip(picked, sums):
                 pairs[p] = x
 
+        @pl.when(relay_turn)
+        def _():
+            arrived(relay_in, relay_sem)
+            for e in range(2):
+                start(*relay_copy(e))
+
+        def edge_up():
+            extra_out[0] = near * pairs[0] - far * pairs[1]
+            start(extra_out.at[0], extra_in.at[s], extra_sem, device(ring + 1, 0, yo, co))
+
+        def now(q, *picked):
+            pair_sums(q, picked)
+            edge_up()
+
         for q in order[:3]:
-            arrived(late.at[q], late_sem.at[q])
+            arrived(late.at[q, pl.ds(2, 2)], edge_sem.at[q])
+            arrived(late.at[q, 0], same_sem.at[q])
+            arrived(late.at[q, 1], cross_sem.at[q])
             pair_sums(q, range(8))
             y_current(late, q, 0, 1)
             y_current(late, q, 1, 2)
         q = order[3]
-        arrived(late.at[q], late_sem.at[q])
-        pair_sums(q, range(3))
-        b1n0, b0n0, p1a1 = (pairs[p] for p in range(3))
-        extra_out[0] = near * b1n0 - far * b0n0
+        arrived(late.at[q, pl.ds(2, 2)], edge_sem.at[q])
+        pl.when(ahead)(lambda: now(q, 0))
+        arrived(late.at[q, 0], same_sem.at[q])
+        arrived(late.at[q, 1], cross_sem.at[q])
+        pl.when(ahead)(lambda: pair_sums(q, (1,)))
+        pl.when(jnp.logical_not(ahead))(lambda: now(q, 0, 1))
+        pair_sums(q, (2,))
+        b1n0, b0n0, p1a1 = pairs[0], pairs[1], -pairs[2]
         extra_out[1] = -far * p1a1
-        for e, r in ((0, ring + 1), (1, ring - 1)):
-            send(extra_out.at[e], extra_in.at[s], extra_sem, device(r, e, yo, co))
+        send(extra_out.at[1], extra_in.at[s], extra_sem, device(ring - 1, 1, yo, co))
         pair_sums(q, range(3, 8))
-        a01, a1b0, b01, a0b0, a1b1 = (pairs[p] for p in range(3, 8))
+        a01, a1b0, b01, a0b0, a1b1 = -pairs[3], pairs[4], pairs[5], -pairs[6], pairs[7]
         main_out[0, 0] = near * a01 - far * a0b0
         main_out[0, 1] = near * (a1b0 + a01) - far * (a1b1 + p1a1)
         main_out[1, 0] = near * (b01 + a1b0) - far * (b0n0 + a0b0)
@@ -198,6 +245,19 @@
         for e in range(2):
             main_out[e, 3] = far * y_acc[1 + e]
             to_owner(e, 3, 1)
+
+        @pl.when(early)
+        def _():
+            arrived(tip_in, tip_sem)
+
+            def step(n, total):
+                w = weights[q, pl.ds(n, 1), :]
+                here = [w * outer[q, 0, n, p].astype(F32) for p in range(2)]
+                there = [tip_in[n, p].astype(F32) for p in range(2)]
+                return total + term(there, here)
+
+            extra_out[2] = -far * lax.fori_loop(0, bands, step, jnp.zeros((16, 128), F32), unroll=4)
+            start(*sums_copy())
 
         arrived(x_in.at[pl.ds(0, 3)], x_sem)
         total = x_acc[:, pl.ds(pl.multiple_of(32 * b, 32), 32), :]
@@ -212,6 +272,28 @@
             out[2, s, rows, :] = main_in[h, 2]
             out[2, 1 - s, rows, :] = main_in[h, 3]
             out[0, s, rows, :] += extra_in[h]
+
+        @pl.when(early & (s == 0))
+        def _():
+            arrived(tip_sums, sums_sem)
+            for h in range(2):
+                out[0, 0, 16 * h : 16 * h + 16, :] += tip_sums[h]
+
+        def sent_copy(src, dst, sem, target):
+            pltpu.make_async_remote_copy(
+                src_ref=src, dst_ref=dst, send_sem=send_sem, recv_sem=sem, device_id=target, device_id_type=MESH
+            ).wait_send()
+
+        sent_copy(extra_out.at[0], extra_in.at[s], extra_sem, device(ring + 1, 0, yo, co))
+
+        pl.when(early)(lambda: sent_copy(*sums_copy()))
+        for turn_, copies in ((tip_turn, tip_copy), (relay_turn, relay_copy)):
+
+            @pl.when(turn_)
+            def _():
+                for e in range(2):
+                    sent_copy(*copies(e))
+
         for copy in sent:
             copy.wait_send()
 
@@ -244,9 +326,12 @@
                 pltpu.VMEM((8, 16, 128), F32),
                 pltpu.VMEM((2, 4, 16, 128), F32),
                 pltpu.VMEM((2, 4, 16, 128), F32),
+                pltpu.VMEM((3, 16, 128), F32),
                 pltpu.VMEM((2, 16, 128), F32),
+                pltpu.VMEM(chunk, BF16),
+                pltpu.VMEM((2, *chunk), BF16),
                 pltpu.VMEM((2, 16, 128), F32),
-                dma, dma((2,)), dma, dma((4,)), dma((4,)), dma, dma, dma, dma,
+                dma, dma((2,)), dma, dma((4,)), dma((4,)), dma((4,)), dma((4,)), dma, dma, dma, dma, dma, dma, dma,
                 pltpu.SemaphoreType.REGULAR, pltpu.SemaphoreType.REGULAR,
             ],
             compiler_params=pltpu.CompilerParams(collective_id=0, has_side_effects=True),

time: 38.9 us -> 37.1 us (0.954)
  Pallas kernels: 38.1 us -> 36.4 us
    pallas_call x1, Pallas kernels: 38.1 us -> 36.4 us  [per_device(): pl.pallas_call(make_kernel(rings), out_shape=pltpu.VMEM((3, 2, 32, 128),...]
where the time goes in v5:
time: 37.1 us; the launch traced here: 37 us
  Pallas kernels  36.4 us (98%)
  local copies, waits for them, and re-layouts  0.64 us (2%)
    pallas_call x1, Pallas kernels, per_device(): pl.pallas_call(make_kernel(rings), out_shape=pltpu.VMEM((3, 2, 32, 128),...  36.4 us

profile of v5, /device:TPU:1, one launch (start us, length us, event | category | flops | bytes accessed | tf_op | source)
XLA Modules:
  0.0 37.0 jit_solution(9637448563989163930)
XLA Ops:
  0.0 36.4 %shard_map.28 = f32[3,2,32,128]{3,2,1,0:T(8,128)S(1)} custom-call(bf16[16,2,2,128,128]{4,3,2,1,0:T(8,128)(2,1)} %orb.1, f32[16]{0:T(128)} %occ_in.1), custom_call_target="tpu_custom_call" | custom-call | tf_op jit(solution)/shard_map/pallas_call | solution.py:310
  36.4 0.6 %copy.4 = f32[3,2,32,128]{3,2,1,0:T(8,128)} copy(f32[3,2,32,128]{3,2,1,0:T(8,128)S(1)} %shard_map.28) | data formatting | bytes 196608

commit v6 on v5

--- a/solution.py
+++ b/solution.py
@@ -20,7 +20,11 @@
     return (near + far).astype(BF16)
 
 
-INNER = [(0, 0, 1), (1, 0, 0), (1, 0, 1), (0, 1, 0), (1, 1, 0), (0, 1, 1), (1, 1, 1)]
+OUTER = [(0, 0, 1), (1, 0, 0), (1, 0, 1), (0, 1, 0), (1, 1, 0), (0, 1, 1), (1, 1, 1)]
+INNER = [(0, 0, 1), (0, 1, 0), (1, 1, 0), (0, 1, 1), (1, 1, 1), (1, 0, 0), (1, 0, 1)]
+OUTER_USE = [(0, 0), (0, 1), (1, 0), (1, 1)]
+INNER_USE = [(1, 0), (1, 1), (0, 0), (0, 1)]
+SAME_USE = [(0, 0), (0, 1), (1, 0), (1, 1)]
 
 
 def EARLY(ring, rings):
@@ -46,8 +50,7 @@
         def device(r, s_, yl_, c_):
             return {"band": 2 * yl_ + c_, "grid": 2 * ((r + rings) % rings) + s_}
 
-        flips = [(0, 0, 1), (1, 0, 0), (1, 0, 1), (0, 1, 0), (1, 1, 0), (0, 1, 1), (1, 1, 1)]
-        peers = [((s + i) % 2, (yl + j) % 2, (c + k) % 2) for i, j, k in flips]
+        peers = [((s + i) % 2, (yl + j) % 2, (c + k) % 2) for i, j, k in OUTER]
         above, below = device(ring + 1, s, yl, c), device(ring - 1, s, yl, c)
         barrier = pltpu.get_barrier_semaphore()
 
@@ -104,20 +107,22 @@
 
         for j, i in [(0, 1), (1, 0), (1, 1)]:
             send(weights.at[b], weights.at[b], weight_sem, device(ring, s, (yl + j) % 2, (c + i) % 2))
-        def tip_copy(e):
-            return (own.at[:, :, 0, my_rows(e, yo, co), :], relay_in.at[e], relay_sem, above)
+        late_j, late_i = INNER_USE[3]
+        yt, ct = (yl + late_j) % 2, (c + late_i) % 2
+
+        def tip_copy():
+            return (own.at[:, :, 0, my_rows(0, yt, ct), :], relay_in, relay_sem, above)
 
         def sums_copy():
-            return (extra_out.at[2], tip_sums.at[s], sums_sem, device(ring, 0, yo, co))
-
-        def relay_copy(e):
-            return (relay_in.at[e], tip_in, tip_sem, device(ring, e, yo, co))
+            return (extra_out.at[2], tip_sums, sums_sem, device(ring, 0, yo, co))
+
+        def relay_copy():
+            return (relay_in, tip_in, tip_sem, device(ring, 0, yt, ct))
 
         @pl.when(tip_turn)
         def _():
             loads[1].wait()
-            for e in range(2):
-                start(*tip_copy(e))
+            start(*tip_copy())
 
         for s_, yl_, c_ in peers:
             send(own.at[:, :, s, my_rows(s_, yl_, c_), :], outer.at[b, s], outer_sem.at[b], device(ring, s_, yl_, c_))
@@ -160,9 +165,12 @@
                 total = total + weights[q, n : n + 1, :] * (re * dim - im * dre)
             y_acc[plane] = total
 
-        order = [2 * ((yl + j) % 2) + (c + i) % 2 for j, i in [(0, 0), (0, 1), (1, 0), (1, 1)]]
-
-        for q in order:
+        def groups(flips):
+            return [2 * ((yl + j) % 2) + (c + i) % 2 for j, i in flips]
+
+        order = groups(INNER_USE)
+
+        for q in groups(OUTER_USE):
             arrived(outer.at[q], outer_sem.at[q])
             send(outer.at[q, 0], late.at[q, 2], edge_sem.at[q], below)
             send(outer.at[q, 1], late.at[q, 3], edge_sem.at[q], above)
@@ -203,36 +211,57 @@
         @pl.when(relay_turn)
         def _():
             arrived(relay_in, relay_sem)
-            for e in range(2):
-                start(*relay_copy(e))
+            start(*relay_copy())
 
         def edge_up():
             extra_out[0] = near * pairs[0] - far * pairs[1]
             start(extra_out.at[0], extra_in.at[s], extra_sem, device(ring + 1, 0, yo, co))
 
-        def now(q, *picked):
-            pair_sums(q, picked)
-            edge_up()
-
-        for q in order[:3]:
+        def edge_down():
+            extra_out[1] = far * pairs[2]
+            start(extra_out.at[1], extra_in.at[s], extra_sem, device(ring - 1, 1, yo, co))
+
+        def inner_y(e):
+            main_out[e, 3] = far * y_acc[1 + e]
+            to_owner(e, 3, 1)
+
+        for q in groups(SAME_USE):
             arrived(late.at[q, pl.ds(2, 2)], edge_sem.at[q])
             arrived(late.at[q, 0], same_sem.at[q])
-            arrived(late.at[q, 1], cross_sem.at[q])
-            pair_sums(q, range(8))
-            y_current(late, q, 0, 1)
-            y_current(late, q, 1, 2)
-        q = order[3]
-        arrived(late.at[q, pl.ds(2, 2)], edge_sem.at[q])
-        pl.when(ahead)(lambda: now(q, 0))
-        arrived(late.at[q, 0], same_sem.at[q])
-        arrived(late.at[q, 1], cross_sem.at[q])
-        pl.when(ahead)(lambda: pair_sums(q, (1,)))
-        pl.when(jnp.logical_not(ahead))(lambda: now(q, 0, 1))
-        pair_sums(q, (2,))
+            pl.when(s == 0)(lambda: pair_sums(q, (2,)))
+            pl.when(s == 1)(lambda: pair_sums(q, (0, 1)))
+            y_current(late, q, s, 1 + s)
+        pl.when(s == 0)(edge_down)
+        pl.when(s == 1)(edge_up)
+        inner_y(s)
+
+        for k, q in enumerate(order):
+            arrived(late.at[q, 0], cross_sem.at[q])
+
+            @pl.when(s == 1)
+            def _():
+                pair_sums(q, (2,))
+                if k == 3:
+                    edge_down()
+
+            @pl.when((s == 0) & jnp.logical_not(ahead))
+            def _():
+                pair_sums(q, (0, 1))
+                if k == 3:
+                    edge_up()
+
+            @pl.when((s == 0) & ahead)
+            def _():
+                pair_sums(q, (0, 1) if k < 3 else (1,))
+                if k == 2:
+                    pair_sums(order[3], (0,))
+                    edge_up()
+
+            pair_sums(q, range(3, 8))
+            if k < 3:
+                y_current(late, q, 1 - s, 2 - s)
+
         b1n0, b0n0, p1a1 = pairs[0], pairs[1], -pairs[2]
-        extra_out[1] = -far * p1a1
-        send(extra_out.at[1], extra_in.at[s], extra_sem, device(ring - 1, 1, yo, co))
-        pair_sums(q, range(3, 8))
         a01, a1b0, b01, a0b0, a1b1 = -pairs[3], pairs[4], pairs[5], -pairs[6], pairs[7]
         main_out[0, 0] = near * a01 - far * a0b0
         main_out[0, 1] = near * (a1b0 + a01) - far * (a1b1 + p1a1)
@@ -240,14 +269,12 @@
         main_out[1, 1] = near * (b1n0 + b01) - far * a1b1
         for e in range(2):
             to_owner(e, 0, 2)
-        y_current(late, q, 0, 1)
-        y_current(late, q, 1, 2)
-        for e in range(2):
-            main_out[e, 3] = far * y_acc[1 + e]
-            to_owner(e, 3, 1)
-
-        @pl.when(early)
+        y_current(late, order[3], 1 - s, 2 - s)
+        inner_y(1 - s)
+
+        @pl.when(early & (s == 0))
         def _():
+            q = order[3]
             arrived(tip_in, tip_sem)
 
             def step(n, total):
@@ -276,8 +303,7 @@
         @pl.when(early & (s == 0))
         def _():
             arrived(tip_sums, sums_sem)
-            for h in range(2):
-                out[0, 0, 16 * h : 16 * h + 16, :] += tip_sums[h]
+            out[0, 0, :16, :] += tip_sums[...]
 
         def sent_copy(src, dst, sem, target):
             pltpu.make_async_remote_copy(
@@ -285,15 +311,10 @@
             ).wait_send()
 
         sent_copy(extra_out.at[0], extra_in.at[s], extra_sem, device(ring + 1, 0, yo, co))
-
-        pl.when(early)(lambda: sent_copy(*sums_copy()))
-        for turn_, copies in ((tip_turn, tip_copy), (relay_turn, relay_copy)):
-
-            @pl.when(turn_)
-            def _():
-                for e in range(2):
-                    sent_copy(*copies(e))
-
+        sent_copy(extra_out.at[1], extra_in.at[s], extra_sem, device(ring - 1, 1, yo, co))
+        pl.when(early & (s == 0))(lambda: sent_copy(*sums_copy()))
+        pl.when(tip_turn)(lambda: sent_copy(*tip_copy()))
+        pl.when(relay_turn)(lambda: sent_copy(*relay_copy()))
         for copy in sent:
             copy.wait_send()
 
@@ -329,8 +350,8 @@
                 pltpu.VMEM((3, 16, 128), F32),
                 pltpu.VMEM((2, 16, 128), F32),
                 pltpu.VMEM(chunk, BF16),
-                pltpu.VMEM((2, *chunk), BF16),
-                pltpu.VMEM((2, 16, 128), F32),
+                pltpu.VMEM(chunk, BF16),
+                pltpu.VMEM((16, 128), F32),
                 dma, dma((2,)), dma, dma((4,)), dma((4,)), dma((4,)), dma((4,)), dma, dma, dma, dma, dma, dma, dma,
                 pltpu.SemaphoreType.REGULAR, pltpu.SemaphoreType.REGULAR,
             ],

time: 37.1 us -> 36.3 us (0.978)
  Pallas kernels: 36.4 us -> 35.6 us
    pallas_call x1, Pallas kernels: 36.4 us -> 35.6 us  [per_device(): pl.pallas_call(make_kernel(rings), out_shape=pltpu.VMEM((3, 2, 32, 128),...]
where the time goes in v6:
time: 36.3 us; the launch traced here: 36.2 us
  Pallas kernels  35.6 us (98%)
  local copies, waits for them, and re-layouts  0.64 us (2%)
    pallas_call x1, Pallas kernels, per_device(): pl.pallas_call(make_kernel(rings), out_shape=pltpu.VMEM((3, 2, 32, 128),...  35.6 us

profile of v6, /device:TPU:1, one launch (start us, length us, event | category | flops | bytes accessed | tf_op | source)
XLA Modules:
  0.0 36.2 jit_solution(1873866339223419877)
XLA Ops:
  0.0 35.6 %shard_map.28 = f32[3,2,32,128]{3,2,1,0:T(8,128)S(1)} custom-call(bf16[16,2,2,128,128]{4,3,2,1,0:T(8,128)(2,1)} %orb.1, f32[16]{0:T(128)} %occ_in.1), custom_call_target="tpu_custom_call" | custom-call | tf_op jit(solution)/shard_map/pallas_call | solution.py:331
  35.6 0.6 %copy.4 = f32[3,2,32,128]{3,2,1,0:T(8,128)} copy(f32[3,2,32,128]{3,2,1,0:T(8,128)S(1)} %shard_map.28) | data formatting | bytes 196608

commit v7 on v6

--- a/solution.py
+++ b/solution.py
@@ -44,7 +44,7 @@
         g = lax.axis_index("grid")
         ring, s = g // 2, g % 2
         yl, c = b // 2, b % 2
-        yo, co = 1 - yl, 1 - c
+        yo, co = 1 - yl, c
         turn = ring % 4
 
         def device(r, s_, yl_, c_):
@@ -74,7 +74,7 @@
         loads[1].start()
 
         def my_rows(s_, yl_, c_):
-            return pl.ds(pl.multiple_of(32 * (2 * (1 - yl_) + 1 - c_) + 16 * s_, 16), 16)
+            return pl.ds(pl.multiple_of(32 * (2 * (1 - yl_) + c_) + 16 * s_, 16), 16)
 
         mine = my_rows(s, yl, c)
         pltpu.make_async_copy(orb.at[:, :, s, mine, :], outer.at[b, s], outer_sem.at[b]).start()
@@ -148,10 +148,6 @@
             s_, yl_, c_ = (s + i) % 2, (yl + j) % 2, (c + k) % 2
             sem = (cross_sem if i else same_sem).at[b]
             send(own.at[:, :, 1 - s, my_rows(s_, yl_, c_), :], late.at[b, s], sem, device(ring, s_, yl_, c_))
-        for j in range(1, 4):
-            to = (b + j) % 4
-            rows = pl.ds(pl.multiple_of(32 * to, 32), 32)
-            send(x_acc.at[:, rows, :], x_in.at[b], x_sem, device(ring, s, to // 2, to % 2))
 
         arrived(weights.at[pl.ds(0, 3)], weight_sem)
 
@@ -213,6 +209,11 @@
             arrived(relay_in, relay_sem)
             start(*relay_copy())
 
+        for j in range(1, 4):
+            to = (b + j) % 4
+            rows = pl.ds(pl.multiple_of(32 * to, 32), 32)
+            send(x_acc.at[:, rows, :], x_in.at[b], x_sem, device(ring, s, to // 2, to % 2))
+
         def edge_up():
             extra_out[0] = near * pairs[0] - far * pairs[1]
             start(extra_out.at[0], extra_in.at[s], extra_sem, device(ring + 1, 0, yo, co))
@@ -253,8 +254,9 @@
             @pl.when((s == 0) & ahead)
             def _():
                 pair_sums(q, (0, 1) if k < 3 else (1,))
+                if k == 1:
+                    pair_sums(order[3], (0,))
                 if k == 2:
-                    pair_sums(order[3], (0,))
                     edge_up()
 
             pair_sums(q, range(3, 8))

time: 36.3 us -> 35.4 us (0.975)
  Pallas kernels: 35.6 us -> 34.6 us
    pallas_call x1, Pallas kernels: 35.6 us -> 34.6 us  [per_device(): pl.pallas_call(make_kernel(rings), out_shape=pltpu.VMEM((3, 2, 32, 128),...]
where the time goes in v7:
time: 35.4 us; the launch traced here: 35.3 us
  Pallas kernels  34.6 us (98%)
  local copies, waits for them, and re-layouts  0.64 us (2%)
    pallas_call x1, Pallas kernels, per_device(): pl.pallas_call(make_kernel(rings), out_shape=pltpu.VMEM((3, 2, 32, 128),...  34.6 us

profile of v7, /device:TPU:1, one launch (start us, length us, event | category | flops | bytes accessed | tf_op | source)
XLA Modules:
  0.0 35.3 jit_solution(1497513269178409425)
XLA Ops:
  0.0 34.6 %shard_map.28 = f32[3,2,32,128]{3,2,1,0:T(8,128)S(1)} custom-call(bf16[16,2,2,128,128]{4,3,2,1,0:T(8,128)(2,1)} %orb.1, f32[16]{0:T(128)} %occ_in.1), custom_call_target="tpu_custom_call" | custom-call | tf_op jit(solution)/shard_map/pallas_call | solution.py:333
  34.6 0.6 %copy.4 = f32[3,2,32,128]{3,2,1,0:T(8,128)} copy(f32[3,2,32,128]{3,2,1,0:T(8,128)S(1)} %shard_map.28) | data formatting | bytes 196608

commit v8 on v7

--- a/solution.py
+++ b/solution.py
@@ -20,7 +20,7 @@
     return (near + far).astype(BF16)
 
 
-OUTER = [(0, 0, 1), (1, 0, 0), (1, 0, 1), (0, 1, 0), (1, 1, 0), (0, 1, 1), (1, 1, 1)]
+OUTER = [(1, 0, 0), (1, 0, 1), (0, 0, 1), (0, 1, 0), (1, 1, 0), (0, 1, 1), (1, 1, 1)]
 INNER = [(0, 0, 1), (0, 1, 0), (1, 1, 0), (0, 1, 1), (1, 1, 1), (1, 0, 0), (1, 0, 1)]
 OUTER_USE = [(0, 0), (0, 1), (1, 0), (1, 1)]
 INNER_USE = [(1, 0), (1, 1), (0, 0), (0, 1)]
@@ -35,8 +35,8 @@
     def kernel(
         orb, occ_in, out,
         occ, own, outer, late, weights, mat_x, mat_y,
-        x_acc, x_in, y_acc, pairs, main_out, main_in, extra_out, extra_in, tip_in, relay_in, tip_sums,
-        occ_sem, load_sem, send_sem, outer_sem, edge_sem, same_sem, cross_sem, weight_sem, x_sem, main_sem, extra_sem, tip_sem, relay_sem, sums_sem,
+        x_acc, x_in, y_acc, pairs, main_out, main_in, extra_out, extra_in, tip_in, relay_in,
+        occ_sem, load_sem, send_sem, outer_sem, edge_sem, same_sem, cross_sem, weight_sem, x_sem, main_sem, extra_sem, tip_sem, relay_sem,
         up_ready, down_ready,
     ):
         bands = own.shape[0]
@@ -44,7 +44,10 @@
         g = lax.axis_index("grid")
         ring, s = g // 2, g % 2
         yl, c = b // 2, b % 2
-        yo, co = 1 - yl, c
+        def half(s_, yl_):
+            return yl_ + s_ - 2 * s_ * yl_
+
+        yo, co = half(s, yl), c
         turn = ring % 4
 
         def device(r, s_, yl_, c_):
@@ -52,6 +55,9 @@
 
         peers = [((s + i) % 2, (yl + j) % 2, (c + k) % 2) for i, j, k in OUTER]
         above, below = device(ring + 1, s, yl, c), device(ring - 1, s, yl, c)
+        def my_rows(s_, yl_, c_):
+            return pl.ds(pl.multiple_of(32 * (2 * half(s_, yl_) + c_) + 16 * s_, 16), 16)
+
         barrier = pltpu.get_barrier_semaphore()
 
         def signal(sem, target):
@@ -65,16 +71,12 @@
         tip_turn, relay_turn = ahead & (s == 1), early & (s == 1)
 
         occ_load = pltpu.make_async_copy(occ_in, occ, occ_sem)
-        loads = [
-            pltpu.make_async_copy(orb.at[:, :, plane], own.at[:, :, plane], load_sem.at[k])
-            for k, plane in enumerate((s, 1 - s))
-        ]
-        loads[0].start()
-        occ_load.start()
-        loads[1].start()
-
-        def my_rows(s_, yl_, c_):
-            return pl.ds(pl.multiple_of(32 * (2 * (1 - yl_) + c_) + 16 * s_, 16), 16)
+        loads = []
+        for k, (plane, row, rows) in enumerate(((s, 64 * half(1 - s, yl), 64), (s, 64 * yo, 64), (1 - s, 0, 128))):
+            at = pl.ds(pl.multiple_of(row, 64), rows)
+            loads.append(pltpu.make_async_copy(orb.at[:, :, plane, at, :], own.at[:, :, plane, at, :], load_sem.at[k]))
+        for load in (loads[0], loads[1], occ_load, loads[2]):
+            load.start()
 
         mine = my_rows(s, yl, c)
         pltpu.make_async_copy(orb.at[:, :, s, mine, :], outer.at[b, s], outer_sem.at[b]).start()
@@ -113,22 +115,21 @@
         def tip_copy():
             return (own.at[:, :, 0, my_rows(0, yt, ct), :], relay_in, relay_sem, above)
 
-        def sums_copy():
-            return (extra_out.at[2], tip_sums, sums_sem, device(ring, 0, yo, co))
-
         def relay_copy():
             return (relay_in, tip_in, tip_sem, device(ring, 0, yt, ct))
 
         @pl.when(tip_turn)
         def _():
-            loads[1].wait()
+            loads[2].wait()
             start(*tip_copy())
 
-        for s_, yl_, c_ in peers:
+        for k, (s_, yl_, c_) in enumerate(peers):
+            if k == 2:
+                loads[1].wait()
             send(own.at[:, :, s, my_rows(s_, yl_, c_), :], outer.at[b, s], outer_sem.at[b], device(ring, s_, yl_, c_))
         pl.when(turn != 0)(lambda: signal(up_ready, below))
         pl.when(turn == 3)(lambda: signal(down_ready, above))
-        pl.when(jnp.logical_not(tip_turn))(lambda: loads[1].wait())
+        pl.when(jnp.logical_not(tip_turn))(lambda: loads[2].wait())
 
         def x_step(n, _):
             w = occ[n]
@@ -173,13 +174,24 @@
             y_current(outer, q, 0, 0)
             y_current(outer, q, 1, 3)
 
+        def main_copy(e, part, size):
+            at = pl.ds(part, size)
+            return (main_out.at[e, at], main_in.at[s, at], main_sem, device(ring, e, yo, co))
+
         def to_owner(e, part, size):
-            send(main_out.at[e, pl.ds(part, size)], main_in.at[s, pl.ds(part, size)], main_sem, device(ring, e, yo, co))
+            if e == 1:
+                start(*main_copy(e, part, size))
+                return
+
+            @pl.when(s == 1)
+            def _():
+                start(*main_copy(e, part, size))
+
+            @pl.when(s == 0)
+            def _():
+                main_in[0, part : part + size] = main_out[0, part : part + size]
 
         near, far = 8.0 / 12.0, 1.0 / 12.0
-        for e in range(2):
-            main_out[e, 2] = far * y_acc[3 * e]
-            to_owner(e, 2, 1)
 
         def term(u, v):
             return u[0] * v[1] - u[1] * v[0]
@@ -214,6 +226,10 @@
             rows = pl.ds(pl.multiple_of(32 * to, 32), 32)
             send(x_acc.at[:, rows, :], x_in.at[b], x_sem, device(ring, s, to // 2, to % 2))
 
+        for e in range(2):
+            main_out[e, 2] = far * y_acc[3 * e]
+            to_owner(e, 2, 1)
+
         def edge_up():
             extra_out[0] = near * pairs[0] - far * pairs[1]
             start(extra_out.at[0], extra_in.at[s], extra_sem, device(ring + 1, 0, yo, co))
@@ -234,7 +250,8 @@
             y_current(late, q, s, 1 + s)
         pl.when(s == 0)(edge_down)
         pl.when(s == 1)(edge_up)
-        inner_y(s)
+        pl.when(s == 0)(lambda: inner_y(0))
+        pl.when(s == 1)(lambda: inner_y(1))
 
         for k, q in enumerate(order):
             arrived(late.at[q, 0], cross_sem.at[q])
@@ -272,8 +289,14 @@
         for e in range(2):
             to_owner(e, 0, 2)
         y_current(late, order[3], 1 - s, 2 - s)
-        inner_y(1 - s)
-
+        pl.when(s == 0)(lambda: inner_y(1))
+        pl.when(s == 1)(lambda: inner_y(0))
+
+        arrived(x_in.at[pl.ds(0, 3)], x_sem)
+        total = x_acc[:, pl.ds(pl.multiple_of(32 * b, 32), 32), :]
+        for j in range(1, 4):
+            total = total + x_in[(b + j) % 4]
+        out[1] = total * far
         @pl.when(early & (s == 0))
         def _():
             q = order[3]
@@ -285,15 +308,10 @@
                 there = [tip_in[n, p].astype(F32) for p in range(2)]
                 return total + term(there, here)
 
-            extra_out[2] = -far * lax.fori_loop(0, bands, step, jnp.zeros((16, 128), F32), unroll=4)
-            start(*sums_copy())
-
-        arrived(x_in.at[pl.ds(0, 3)], x_sem)
-        total = x_acc[:, pl.ds(pl.multiple_of(32 * b, 32), 32), :]
-        for j in range(1, 4):
-            total = total + x_in[(b + j) % 4]
-        out[1] = total * far
-        arrived(main_in, main_sem)
+            main_in[0, 0] -= far * lax.fori_loop(0, bands, step, jnp.zeros((16, 128), F32), unroll=4)
+
+        pl.when(s == 0)(lambda: arrived(main_in.at[1], main_sem))
+        pl.when(s == 1)(lambda: arrived(main_in, main_sem))
         arrived(extra_in, extra_sem)
         for h in range(2):
             rows = slice(16 * h, 16 * h + 16)
@@ -302,11 +320,6 @@
             out[2, 1 - s, rows, :] = main_in[h, 3]
             out[0, s, rows, :] += extra_in[h]
 
-        @pl.when(early & (s == 0))
-        def _():
-            arrived(tip_sums, sums_sem)
-            out[0, 0, :16, :] += tip_sums[...]
-
         def sent_copy(src, dst, sem, target):
             pltpu.make_async_remote_copy(
                 src_ref=src, dst_ref=dst, send_sem=send_sem, recv_sem=sem, device_id=target, device_id_type=MESH
@@ -314,7 +327,14 @@
 
         sent_copy(extra_out.at[0], extra_in.at[s], extra_sem, device(ring + 1, 0, yo, co))
         sent_copy(extra_out.at[1], extra_in.at[s], extra_sem, device(ring - 1, 1, yo, co))
-        pl.when(early & (s == 0))(lambda: sent_copy(*sums_copy()))
+        for part, size in ((0, 2), (2, 1), (3, 1)):
+            sent_copy(*main_copy(1, part, size))
+
+        @pl.when(s == 1)
+        def _():
+            for part, size in ((0, 2), (2, 1), (3, 1)):
+                sent_copy(*main_copy(0, part, size))
+
         pl.when(tip_turn)(lambda: sent_copy(*tip_copy()))
         pl.when(relay_turn)(lambda: sent_copy(*relay_copy()))
         for copy in sent:
@@ -349,12 +369,11 @@
                 pltpu.VMEM((8, 16, 128), F32),
                 pltpu.VMEM((2, 4, 16, 128), F32),
                 pltpu.VMEM((2, 4, 16, 128), F32),
-                pltpu.VMEM((3, 16, 128), F32),
+                pltpu.VMEM((2, 16, 128), F32),
                 pltpu.VMEM((2, 16, 128), F32),
                 pltpu.VMEM(chunk, BF16),
                 pltpu.VMEM(chunk, BF16),
-                pltpu.VMEM((16, 128), F32),
-                dma, dma((2,)), dma, dma((4,)), dma((4,)), dma((4,)), dma((4,)), dma, dma, dma, dma, dma, dma, dma,
+                dma, dma((3,)), dma, dma((4,)), dma((4,)), dma((4,)), dma((4,)), dma, dma, dma, dma, dma, dma,
                 pltpu.SemaphoreType.REGULAR, pltpu.SemaphoreType.REGULAR,
             ],
             compiler_params=pltpu.CompilerParams(collective_id=0, has_side_effects=True),

time: 35.4 us -> 35.3 us (level)
  the two profiles are of different devices: /device:TPU:1 before, /device:TPU:0 now
where the time goes in v8:
time: 35.3 us; the launch traced here: 35.2 us
  Pallas kernels  34.5 us (98%)
  local copies, waits for them, and re-layouts  0.64 us (2%)
    pallas_call x1, Pallas kernels, per_device(): pl.pallas_call(make_kernel(rings), out_shape=pltpu.VMEM((3, 2, 32, 128),...  34.5 us

profile of v8, /device:TPU:0, one launch (start us, length us, event | category | flops | bytes accessed | tf_op | source)
XLA Modules:
  0.0 35.2 jit_solution(7329672689984169653)
XLA Ops:
  0.0 34.5 %shard_map.28 = f32[3,2,32,128]{3,2,1,0:T(8,128)S(1)} custom-call(bf16[16,2,2,128,128]{4,3,2,1,0:T(8,128)(2,1)} %orb.1, f32[16]{0:T(128)} %occ_in.1), custom_call_target="tpu_custom_call" | custom-call | tf_op jit(solution)/shard_map/pallas_call | solution.py:353
  34.6 0.6 %copy.4 = f32[3,2,32,128]{3,2,1,0:T(8,128)} copy(f32[3,2,32,128]{3,2,1,0:T(8,128)S(1)} %shard_map.28) | data formatting | bytes 196608

commit v9 on v8

--- a/solution.py
+++ b/solution.py
@@ -28,15 +28,15 @@
 
 
 def EARLY(ring, rings):
-    return ring == 0, ring == rings - 1
+    return ring % 4 == 0, ring % 4 == 3
 
 
 def make_kernel(rings):
     def kernel(
         orb, occ_in, out,
         occ, own, outer, late, weights, mat_x, mat_y,
-        x_acc, x_in, y_acc, pairs, main_out, main_in, extra_out, extra_in, tip_in, relay_in,
-        occ_sem, load_sem, send_sem, outer_sem, edge_sem, same_sem, cross_sem, weight_sem, x_sem, main_sem, extra_sem, tip_sem, relay_sem,
+        x_acc, x_in, y_acc, pairs, main_out, main_in, extra_out, extra_in, tip_in, relay_in, tip_two, relay_two,
+        occ_sem, load_sem, send_sem, outer_sem, edge_sem, same_sem, cross_sem, weight_sem, x_sem, main_sem, extra_sem, tip_sem, relay_sem, tip_two_sem, relay_two_sem,
         up_ready, down_ready,
     ):
         bands = own.shape[0]
@@ -69,6 +69,7 @@
         pl.when(turn == 0)(lambda: signal(barrier, below))
         early, ahead = EARLY(ring, rings)
         tip_turn, relay_turn = ahead & (s == 1), early & (s == 1)
+        first, last = (ring == 0) & (c == 0), (ring == rings - 1) & (c == 0)
 
         occ_load = pltpu.make_async_copy(occ_in, occ, occ_sem)
         loads = []
@@ -115,6 +116,12 @@
         def tip_copy():
             return (own.at[:, :, 0, my_rows(0, yt, ct), :], relay_in, relay_sem, above)
 
+        def tip_two_copy():
+            return (own.at[:, :, 0, my_rows(0, yl, c), :], relay_two, relay_two_sem, above)
+
+        def relay_two_copy():
+            return (relay_two, tip_two, tip_two_sem, device(ring, 0, yl, c))
+
         def relay_copy():
             return (relay_in, tip_in, tip_sem, device(ring, 0, yt, ct))
 
@@ -122,6 +129,10 @@
         def _():
             loads[2].wait()
             start(*tip_copy())
+
+            @pl.when(last)
+            def _():
+                start(*tip_two_copy())
 
         for k, (s_, yl_, c_) in enumerate(peers):
             if k == 2:
@@ -221,6 +232,11 @@
             arrived(relay_in, relay_sem)
             start(*relay_copy())
 
+            @pl.when(first)
+            def _():
+                arrived(relay_two, relay_two_sem)
+                start(*relay_two_copy())
+
         for j in range(1, 4):
             to = (b + j) % 4
             rows = pl.ds(pl.multiple_of(32 * to, 32), 32)
@@ -270,11 +286,13 @@
 
             @pl.when((s == 0) & ahead)
             def _():
-                pair_sums(q, (0, 1) if k < 3 else (1,))
+                pair_sums(q, (0, 1) if k < 2 else (1,))
                 if k == 1:
+                    pair_sums(order[2], (0,))
                     pair_sums(order[3], (0,))
+                    pl.when(last)(edge_up)
                 if k == 2:
-                    edge_up()
+                    pl.when(jnp.logical_not(last))(edge_up)
 
             pair_sums(q, range(3, 8))
             if k < 3:
@@ -297,28 +315,26 @@
         for j in range(1, 4):
             total = total + x_in[(b + j) % 4]
         out[1] = total * far
-        @pl.when(early & (s == 0))
-        def _():
-            q = order[3]
-            arrived(tip_in, tip_sem)
+        def tip_current(q, tip, sem):
+            arrived(tip, sem)
 
             def step(n, total):
                 w = weights[q, pl.ds(n, 1), :]
                 here = [w * outer[q, 0, n, p].astype(F32) for p in range(2)]
-                there = [tip_in[n, p].astype(F32) for p in range(2)]
+                there = [tip[n, p].astype(F32) for p in range(2)]
                 return total + term(there, here)
 
             main_in[0, 0] -= far * lax.fori_loop(0, bands, step, jnp.zeros((16, 128), F32), unroll=4)
 
+        pl.when(early & (s == 0))(lambda: tip_current(order[3], tip_in, tip_sem))
+        pl.when(first & (s == 0))(lambda: tip_current(order[2], tip_two, tip_two_sem))
         pl.when(s == 0)(lambda: arrived(main_in.at[1], main_sem))
         pl.when(s == 1)(lambda: arrived(main_in, main_sem))
-        arrived(extra_in, extra_sem)
         for h in range(2):
             rows = slice(16 * h, 16 * h + 16)
             out[0, :, rows, :] = main_in[h, :2]
             out[2, s, rows, :] = main_in[h, 2]
             out[2, 1 - s, rows, :] = main_in[h, 3]
-            out[0, s, rows, :] += extra_in[h]
 
         def sent_copy(src, dst, sem, target):
             pltpu.make_async_remote_copy(
@@ -337,8 +353,14 @@
 
         pl.when(tip_turn)(lambda: sent_copy(*tip_copy()))
         pl.when(relay_turn)(lambda: sent_copy(*relay_copy()))
+        pl.when(tip_turn & last)(lambda: sent_copy(*tip_two_copy()))
+        pl.when(relay_turn & first)(lambda: sent_copy(*relay_two_copy()))
         for copy in sent:
             copy.wait_send()
+
+        arrived(extra_in, extra_sem)
+        for h in range(2):
+            out[0, s, 16 * h : 16 * h + 16, :] += extra_in[h]
 
     return kernel
 
@@ -373,7 +395,9 @@
                 pltpu.VMEM((2, 16, 128), F32),
                 pltpu.VMEM(chunk, BF16),
                 pltpu.VMEM(chunk, BF16),
-                dma, dma((3,)), dma, dma((4,)), dma((4,)), dma((4,)), dma((4,)), dma, dma, dma, dma, dma, dma,
+                pltpu.VMEM(chunk, BF16),
+                pltpu.VMEM(chunk, BF16),
+                dma, dma((3,)), dma, dma((4,)), dma((4,)), dma((4,)), dma((4,)), dma, dma, dma, dma, dma, dma, dma, dma,
                 pltpu.SemaphoreType.REGULAR, pltpu.SemaphoreType.REGULAR,
             ],
             compiler_params=pltpu.CompilerParams(collective_id=0, has_side_effects=True),

time: 35.3 us -> 35 us (level)
  the two profiles are of different devices: /device:TPU:0 before, /device:TPU:1 now
where the time goes in v9:
time: 35 us; the launch traced here: 34.6 us
  Pallas kernels  33.9 us (97%)
  local copies, waits for them, and re-layouts  0.64 us (2%)
    pallas_call x1, Pallas kernels, per_device(): pl.pallas_call(make_kernel(rings), out_shape=pltpu.VMEM((3, 2, 32, 128),...  33.9 us

profile of v9, /device:TPU:1, one launch (start us, length us, event | category | flops | bytes accessed | tf_op | source)
XLA Modules:
  0.0 34.6 jit_solution(13207546655865787137)
XLA Ops:
  0.0 33.9 %shard_map.28 = f32[3,2,32,128]{3,2,1,0:T(8,128)S(1)} custom-call(bf16[16,2,2,128,128]{4,3,2,1,0:T(8,128)(2,1)} %orb.1, f32[16]{0:T(128)} %occ_in.1), custom_call_target="tpu_custom_call" | custom-call | tf_op jit(solution)/shard_map/pallas_call | solution.py:375
  33.9 0.6 %copy.4 = f32[3,2,32,128]{3,2,1,0:T(8,128)} copy(f32[3,2,32,128]{3,2,1,0:T(8,128)S(1)} %shard_map.28) | data formatting | bytes 196608

commit v10 on v9

--- a/solution.py
+++ b/solution.py
@@ -223,7 +223,7 @@
                 scaled = {name: (w * field[name][0], w * field[name][1]) for name in sorted({names[p][0] for p in picked})}
                 return tuple(x + term(scaled[names[p][0]], field[names[p][1]]) for x, p in zip(sums, picked))
 
-            sums = lax.fori_loop(0, bands, z_step, tuple(pairs[p] for p in picked), unroll=4)
+            sums = lax.fori_loop(0, bands, z_step, tuple(pairs[p] for p in picked), unroll=8)
             for p, x in zip(picked, sums):
                 pairs[p] = x
 
@@ -324,7 +324,7 @@
                 there = [tip[n, p].astype(F32) for p in range(2)]
                 return total + term(there, here)
 
-            main_in[0, 0] -= far * lax.fori_loop(0, bands, step, jnp.zeros((16, 128), F32), unroll=4)
+            main_in[0, 0] -= far * lax.fori_loop(0, bands, step, jnp.zeros((16, 128), F32), unroll=8)
 
         pl.when(early & (s == 0))(lambda: tip_current(order[3], tip_in, tip_sem))
         pl.when(first & (s == 0))(lambda: tip_current(order[2], tip_two, tip_two_sem))

time: 35 us -> 34.9 us (level)
  no operation moved by 1% of the time
where the time goes in v10:
time: 34.9 us; the launch traced here: 34.6 us
  Pallas kernels  33.9 us (97%)
  local copies, waits for them, and re-layouts  0.64 us (2%)
    pallas_call x1, Pallas kernels, per_device(): pl.pallas_call(make_kernel(rings), out_shape=pltpu.VMEM((3, 2, 32, 128),...  33.9 us

profile of v10, /device:TPU:1, one launch (start us, length us, event | category | flops | bytes accessed | tf_op | source)
XLA Modules:
  0.0 34.6 jit_solution(8516808097967279893)
XLA Ops:
  0.0 33.9 %shard_map.28 = f32[3,2,32,128]{3,2,1,0:T(8,128)S(1)} custom-call(bf16[16,2,2,128,128]{4,3,2,1,0:T(8,128)(2,1)} %orb.1, f32[16]{0:T(128)} %occ_in.1), custom_call_target="tpu_custom_call" | custom-call | tf_op jit(solution)/shard_map/pallas_call | solution.py:375
  33.9 0.6 %copy.4 = f32[3,2,32,128]{3,2,1,0:T(8,128)} copy(f32[3,2,32,128]{3,2,1,0:T(8,128)S(1)} %shard_map.28) | data formatting | bytes 196608
